TPU v7x, 32 devices: a whole 2x2x4 slice. The times are simulated.
32 devices in a mesh: path: 4 (over y, core), fsdp: 8 (over z, x).
Axes of the slice: x: 2, y: 2, z: 4, core: 2. Of those that a mesh axis runs over, the one named last changes fastest.
Arguments:
- input_activation_matrix: bfloat16 [4, 1536, 2048], P('path', 'fsdp'), may hold values from -6 to 6
- output_sensitivity: bfloat16 [4, 1536, 2048], P('path', 'fsdp'), may hold values from -12 to 12
- trajectory_initial_parameters: bfloat16 [4, 8, 1024, 4096], P('path', None, 'fsdp'), may hold values from -6 to 6
- trajectory_gradient_average: bfloat16 [4, 8, 1024, 4096], P('path', None, 'fsdp'), may hold values from -0.19921875 to 0.19921875
- trajectory_squared_average: bfloat16 [4, 8, 1024, 4096], P('path', None, 'fsdp'), may hold values from 0.0009994507 to 0.099609375
- common_expert_parameters: float32 [8, 2, 1024, 4096], P('path', None, 'fsdp'), may hold values from -6 to 6
- outer_inertia: float32 [8, 2, 1024, 4096], P('path', None, 'fsdp'), may hold values from -0.4 to 0.4
- trajectory_membership: int32 [4, 8], replicated, may hold values from 0 to 1
- punctual_flags: int32 [4], replicated, may hold values 0 or 1
Outputs:
- refreshed_experts: float32 [8, 2, 1024, 4096], P('path', None, 'fsdp')
- refreshed_inertia: float32 [8, 2, 1024, 4096], P('path', None, 'fsdp')
- returned: bfloat16 [4, 8, 1024, 4096], P('path', None, 'fsdp')
All inputs are finite; a program needn't handle non-finite values.
Results may differ from a plain program's by a relative error of at most 0.0024.
Values may be sent and summed in bfloat16 or wider, within the bound.
A program may use at most 320 MiB of HBM per device.

v0:
```python
import functools

import jax
import jax.numpy as jnp
from jax import lax
from jax.experimental import pallas as pl
from jax.experimental.pallas import tpu as pltpu
from jax.sharding import PartitionSpec as P


UNIT = 1024
SETS = 8
STEP = 1000


BETA_ONE = 0.9
BETA_TWO = 0.999
ADAM_EPS = 1e-08
INNER_RATE = 0.05
DECAY = 0.1
GLOBAL_LEARNING = 0.7
INERTIA_FACTOR = 0.9

MESH = pl.DeviceIdType.MESH
GELU_ROOT = 0.7978845608028654
GELU_CUBE = 0.044715


def adam_delta(grads, first, second, start):
    corr_one = 1.0 - BETA_ONE**STEP
    corr_two = 1.0 - BETA_TWO**STEP
    first_new = BETA_ONE * first.astype(jnp.float32) + (1.0 - BETA_ONE) * grads
    second_new = BETA_TWO * second.astype(jnp.float32) + (1.0 - BETA_TWO) * grads * grads
    direction = first_new / corr_one / (jnp.sqrt(second_new / corr_two) + ADAM_EPS)
    return (INNER_RATE * (direction + DECAY * start.astype(jnp.float32))).astype(jnp.bfloat16)


def gelu_pair(pre):
    square = pre * pre
    tanh = jnp.tanh(GELU_ROOT * pre * (1.0 + GELU_CUBE * square))
    half = 0.5 * (1.0 + tanh)
    slope = half + 0.5 * pre * (1.0 - tanh * tanh) * GELU_ROOT * (1.0 + 3.0 * GELU_CUBE * square)
    return pre * half, slope


def divisor(total, wanted):
    size = min(total, wanted)
    while total % size:
        size //= 2
    return size


class Plan:
    def __init__(self, paths, ring, shard, features, rows):
        self.paths, self.ring, self.shard = paths, ring, shard
        self.features, self.width, self.rows = features, 2 * features, rows
        self.tokens = ring * shard
        self.half = shard // 2
        self.owned = rows // paths
        self.group = 1
        while (self.group * shard) % 128:
            self.group *= 2
        self.batch = self.group * shard
        self.tile = divisor(features, 512)
        self.tiles = self.width // self.tile
        self.units = divisor(rows, 256)


def ring_neighbours(index, size):
    odd = index % 2
    rank = (1 - odd) * (index // 2) + odd * (size - (index + 1) // 2)

    def place(r):
        high = r // (size // 2)
        return (1 - high) * 2 * r + high * (2 * (size - r) - 1)

    return place((rank + 1) % size), place((rank + size - 1) % size)


def path_kernel(
    plan, single, flags_ref, x_hbm, g_hbm, r_hbm, m_hbm, v_hbm, arr_hbm, own_hbm, *scratch
):
    (xg, params, hidden, first, second, pseudo) = scratch[:6]
    if single:
        (raw, swapped, cross_in, own_in, cross_out, own_out) = scratch[6:12]
    (load_sem, moment_sem, send_sem, recv_sem, side_send, side_recv, out_send, out_recv, keep_sem) = (
        scratch[-9:]
    )
    n, shard, half = plan.ring, plan.shard, plan.half
    features, owned, tile, tiles = plan.features, plan.owned, plan.tile, plan.tiles
    path = lax.axis_index("path")
    place = lax.axis_index("fsdp")
    ahead, behind = ring_neighbours(place, n)
    core = path % 2
    sibling = path + 1 - 2 * core
    lanes = 1 if single else 2

    barrier = pltpu.get_barrier_semaphore()
    for spot in (ahead, behind):
        pl.semaphore_signal(
            barrier, inc=1, device_id={"path": path, "fsdp": spot}, device_id_type=MESH
        )
    for k in range(1, plan.paths):
        pl.semaphore_signal(
            barrier,
            inc=1,
            device_id={"path": (path + k) % plan.paths, "fsdp": place},
            device_id_type=MESH,
        )

    def moments(t, slot):
        cols = pl.ds(pl.multiple_of(t * tile, tile), tile)
        return (
            pltpu.make_async_copy(m_hbm.at[:, cols], first.at[slot], moment_sem.at[0, slot]),
            pltpu.make_async_copy(v_hbm.at[:, cols], second.at[slot], moment_sem.at[1, slot]),
        )

    if single:
        loads = (
            pltpu.make_async_copy(x_hbm, raw.at[0], load_sem.at[0]),
            pltpu.make_async_copy(g_hbm, raw.at[1], load_sem.at[1]),
        )
    else:
        loads = (
            pltpu.make_async_copy(x_hbm, xg.at[0, pl.ds(0, shard)], load_sem.at[0]),
            pltpu.make_async_copy(g_hbm, xg.at[1, pl.ds(0, shard)], load_sem.at[1]),
        )
    for load in loads:
        load.start()
    load_params = pltpu.make_async_copy(r_hbm, params, load_sem.at[2])
    load_params.start()
    for load in moments(0, 0):
        load.start()
    pl.semaphore_wait(barrier, plan.paths + 1)
    for load in loads:
        load.wait()

    def ring_copy(step, lane, way):
        array = core if single else lane
        source = pl.ds(pl.multiple_of((step - 1) * shard + way * half, half), half)
        target = pl.ds(pl.multiple_of(step * shard + way * half, half), half)
        return pltpu.make_async_remote_copy(
            src_ref=xg.at[array, source],
            dst_ref=xg.at[array, target],
            send_sem=send_sem.at[lane, way, step],
            recv_sem=recv_sem.at[lane, way, step],
            device_id={"path": path, "fsdp": behind if way else ahead},
            device_id_type=MESH,
        )

    def side_copy(slot, array):
        rows = pl.ds(pl.multiple_of(slot * shard, shard), shard)
        return pltpu.make_async_remote_copy(
            src_ref=xg.at[array, rows],
            dst_ref=xg.at[array, rows],
            send_sem=side_send.at[slot],
            recv_sem=side_recv.at[slot],
            device_id={"path": sibling, "fsdp": place},
            device_id_type=MESH,
        )

    if single:
        active = lead_of(flags_ref, path // 2) == path
        swap = pltpu.make_async_remote_copy(
            src_ref=raw.at[1 - core],
            dst_ref=swapped,
            send_sem=load_sem.at[3],
            recv_sem=load_sem.at[4],
            device_id={"path": sibling, "fsdp": place},
            device_id_type=MESH,
        )
        swap.start()
        swap.wait()
        xg[core, 0:shard] = jnp.where(active, raw[core], swapped[...])

    load_params.wait()

    def forward(j):
        rows = pl.ds(pl.multiple_of(j * plan.batch, plan.batch), plan.batch)

        def unit(u, carry):
            strip = pl.ds(pl.multiple_of(u * plan.units, plan.units), plan.units)
            nt = (((1,), (1,)), ((), ()))
            pre = lax.dot_general(
                params[strip, 0:features], xg[0, rows], nt, preferred_element_type=jnp.float32
            ) * (features**-0.5)
            act, slope = gelu_pair(pre)
            hidden[1, strip, rows] = act.astype(jnp.bfloat16)
            back = lax.dot_general(
                params[strip, features : 2 * features],
                xg[1, rows],
                nt,
                preferred_element_type=jnp.float32,
            ) * ((SETS * UNIT) ** -0.5)
            hidden[0, strip, rows] = (back * slope).astype(jnp.bfloat16)
            return carry

        lax.fori_loop(0, plan.rows // plan.units, unit, 0)

    def gather_batch(j, carry):
        for i in range(plan.group):
            k = j * plan.group + i

            @pl.when(k > 0)
            def _():
                for lane in range(lanes):
                    for way in range(2):
                        ring_copy(k, lane, way).wait_recv()

            @pl.when(k < n - 1)
            def _():
                for lane in range(lanes):
                    for way in range(2):
                        ring_copy(k + 1, lane, way).start()

            if single:
                side_copy(k, core).start()
        if single:
            for i in range(plan.group):
                side_copy(j * plan.group + i, 1 - core).wait_recv()
        forward(j)
        return carry

    lax.fori_loop(0, n // plan.group, gather_batch, 0)

    def cols_of(t):
        return pl.ds(pl.multiple_of(t * tile, tile), tile)

    def rows_of(p):
        return pl.ds(pl.multiple_of(p * owned, owned), owned)

    chip = path // 2
    far = (1 - chip) * 2

    def out_copy(t, k):
        owner = (path + k) % plan.paths
        return pltpu.make_async_remote_copy(
            src_ref=pseudo.at[rows_of(owner), cols_of(t)],
            dst_ref=arr_hbm.at[path, :, cols_of(t)],
            send_sem=out_send.at[t, k],
            recv_sem=out_recv.at[t, k],
            device_id={"path": owner, "fsdp": place},
            device_id_type=MESH,
        )

    def keep_copy(t):
        return pltpu.make_async_copy(
            pseudo.at[rows_of(path), cols_of(t)],
            arr_hbm.at[path, :, cols_of(t)],
            keep_sem.at[0, t],
        )

    def share_copy(t, which):
        owner = (far + 1 - core) if which == 0 else sibling
        return pltpu.make_async_remote_copy(
            src_ref=pseudo.at[rows_of(owner), cols_of(t)],
            dst_ref=(cross_in if which == 0 else own_in).at[t],
            send_sem=out_send.at[t, which],
            recv_sem=out_recv.at[t, which],
            device_id={"path": sibling, "fsdp": place},
            device_id_type=MESH,
        )

    def cross_copy(t):
        return pltpu.make_async_remote_copy(
            src_ref=cross_out.at[t],
            dst_ref=arr_hbm.at[chip, :, cols_of(t)],
            send_sem=out_send.at[t, 2],
            recv_sem=out_recv.at[t, 2],
            device_id={"path": far + core, "fsdp": place},
            device_id_type=MESH,
        )

    def near_copy(t):
        return pltpu.make_async_copy(
            own_out.at[t], arr_hbm.at[chip, :, cols_of(t)], keep_sem.at[0, t]
        )

    def late_copy(t):
        return pltpu.make_async_copy(
            pseudo.at[pl.ds(pl.multiple_of(far * owned, 2 * owned), 2 * owned), cols_of(t)],
            own_hbm.at[:, cols_of(t)],
            keep_sem.at[1, t],
        )

    def pick(t):
        share_copy(t, 0).wait_recv()
        cross_out[t] = jnp.where(active, pseudo[rows_of(far + core), cols_of(t)], cross_in[t])
        cross_copy(t).start()
        share_copy(t, 1).wait_recv()
        own_out[t] = jnp.where(active, pseudo[rows_of(path), cols_of(t)], own_in[t])
        near_copy(t).start()

    def grad_tile(t, carry):
        slot = t % 2

        @pl.when(t + 1 < tiles)
        def _():
            for load in moments(t + 1, 1 - slot):
                load.start()

        for load in moments(t, slot):
            load.wait()
        side = t // (tiles // 2)
        scale = jnp.where(side == 0, features**-0.5, (SETS * UNIT) ** -0.5).astype(jnp.float32)
        token_cols = pl.ds(pl.multiple_of(t % (tiles // 2) * tile, tile), tile)

        def unit(u, inner):
            strip = pl.ds(pl.multiple_of(u * plan.units, plan.units), plan.units)
            grads = (
                jnp.dot(
                    hidden[side, strip, :],
                    xg[side, :, token_cols],
                    preferred_element_type=jnp.float32,
                )
                * scale
            )
            pseudo[strip, cols_of(t)] = adam_delta(
                grads, first[slot, strip, :], second[slot, strip, :], params[strip, cols_of(t)]
            )
            return inner

        lax.fori_loop(0, plan.rows // plan.units, unit, 0)
        if single:
            share_copy(t, 0).start()
            share_copy(t, 1).start()
            late_copy(t).start()

            @pl.when(t > 0)
            def _():
                pick(t - 1)
        else:
            for k in range(plan.paths - 1, 0, -1):
                out_copy(t, k).start()
            keep_copy(t).start()
        return carry

    lax.fori_loop(0, tiles, grad_tile, 0)
    if single:
        pick(tiles - 1)

    def drain_ring(k, carry):
        for lane in range(lanes):
            for way in range(2):
                ring_copy(k, lane, way).wait_send()
        return carry

    lax.fori_loop(1, n, drain_ring, 0)
    if single:

        def drain_side(k, carry):
            side_copy(k, core).wait_send()
            return carry

        lax.fori_loop(0, n, drain_side, 0)

    def drain(t, carry):
        if single:
            share_copy(t, 0).wait_send()
            share_copy(t, 1).wait_send()
            late_copy(t).wait()
            near_copy(t).wait()
            cross_copy(t).wait()
        else:
            for k in range(1, plan.paths):
                out_copy(t, k).wait()
            keep_copy(t).wait()
        return carry

    lax.fori_loop(0, tiles, drain, 0)


def run_path(plan, single, flags, x, g, r, m, v):
    bf16 = jnp.bfloat16
    width, tile, tiles = plan.width, plan.tile, plan.tiles
    scratch = [
        pltpu.VMEM((2, plan.tokens, plan.features), bf16),
        pltpu.VMEM((plan.rows, width), bf16),
        pltpu.VMEM((2, plan.rows, plan.tokens), bf16),
        pltpu.VMEM((2, plan.rows, tile), bf16),
        pltpu.VMEM((2, plan.rows, tile), bf16),
        pltpu.VMEM((plan.rows, width), bf16),
    ]
    if single:
        scratch += [
            pltpu.VMEM((2, plan.shard, plan.features), bf16),
            pltpu.VMEM((plan.shard, plan.features), bf16),
        ] + [pltpu.VMEM((tiles, plan.owned, tile), bf16)] * 4
    lanes = 1 if single else 2
    outs = 3 if single else plan.paths
    dma = pltpu.SemaphoreType.DMA
    scratch += [
        dma((5,)),
        dma((2, 2)),
        dma((lanes, 2, plan.ring)),
        dma((lanes, 2, plan.ring)),
        dma((plan.ring,)),
        dma((plan.ring,)),
        dma((tiles, outs)),
        dma((tiles, outs)),
        dma((2, tiles)),
    ]
    sources = 2 if single else plan.paths
    flops = 8 * plan.tokens * plan.features * plan.rows
    shapes = [jax.ShapeDtypeStruct((sources, plan.owned, width), bf16)]
    if single:
        shapes.append(jax.ShapeDtypeStruct((2 * plan.owned, width), bf16))
    body = functools.partial(path_kernel, plan, single)
    if not single:
        inner = body

        def body(flags_ref, x, g, r, m, v, arr, *rest):
            inner(flags_ref, x, g, r, m, v, arr, None, *rest)

    anywhere = pl.BlockSpec(memory_space=pl.ANY)
    return pl.pallas_call(
        body,
        out_shape=shapes,
        in_specs=[pl.BlockSpec(memory_space=pltpu.SMEM)] + [anywhere] * 5,
        out_specs=[anywhere] * len(shapes),
        scratch_shapes=scratch,
        compiler_params=pltpu.CompilerParams(
            collective_id=0 if single else 1,
            has_side_effects=True,
            vmem_limit_bytes=63 * 1024 * 1024,
        ),
        cost_estimate=pl.CostEstimate(
            flops=flops, bytes_accessed=8 * plan.rows * width, transcendentals=0
        ),
        name="single_path" if single else "both_paths",
    )(flags, x, g, r, m, v)


def refreshed(total, tally, common, inertia):
    average = total / tally
    inertia = INERTIA_FACTOR * inertia + average
    expert = common - GLOBAL_LEARNING * (average + INERTIA_FACTOR * inertia)
    return expert, inertia


def lead_of(flags_ref, chip):
    return 2 * chip + jnp.where(flags_ref[2 * chip + 1] == 1, 1, 0)


def late_of(member_ref, flags_ref, at, owner_chip):
    far = 2 * (1 - owner_chip)
    near = member_ref[lead_of(flags_ref, owner_chip), at]
    shared = member_ref[far, at]
    return jnp.where(shared == member_ref[far + 1, at], shared, near)


def local_call(body, grid, in_specs, out_specs, out_shape, scalars, arrays, aliases=None):
    size = sum(array.size * array.dtype.itemsize for array in arrays)
    return pl.pallas_call(
        body,
        grid_spec=pltpu.PrefetchScalarGridSpec(
            num_scalar_prefetch=len(scalars), grid=grid, in_specs=in_specs, out_specs=out_specs
        ),
        out_shape=out_shape,
        input_output_aliases=aliases or {},
        compiler_params=pltpu.CompilerParams(vmem_limit_bytes=56 * 1024 * 1024),
        cost_estimate=pl.CostEstimate(flops=size, bytes_accessed=size, transcendentals=0),
    )(*scalars, *arrays)


ANYWHERE = pl.BlockSpec(memory_space=pl.ANY)


def pick_early(scalars, common, inertia):
    sets, _, units, width = common.shape
    step = divisor(width, 2048)

    def body(member_ref, flags_ref, spot_ref, common_ref, inertia_ref, out):
        expert, _ = refreshed(0.0, 1.0, common_ref[0, 0], inertia_ref[0, 0])
        out[0] = expert.astype(jnp.bfloat16)

    def at(j, t, member_ref, flags_ref, spot_ref):
        spot = spot_ref[0]
        late = late_of(member_ref, flags_ref, spot * sets + j, spot // 2)
        return (j, 1 - late, 0, t)

    return local_call(
        body,
        (sets, width // step),
        [pl.BlockSpec((1, 1, units, step), at)] * 2,
        pl.BlockSpec((1, units, step), lambda j, t, *_: (j, 0, t)),
        jax.ShapeDtypeStruct((sets, units, width), jnp.bfloat16),
        scalars,
        [common, inertia],
    )


def finish_set(scalars, common, inertia, arrived, j, single, paths, shape, partial):
    sets, choices, units, width = common.shape
    sources = arrived.shape[0]
    step = divisor(width, 1024)
    sends = 2 if single else paths - 1

    def body(member_ref, flags_ref, spot_ref, shares, common_ref, inertia_ref, *refs):
        expert_out, inertia_out, returned, *outs = refs[-3 - sends :]
        spot = spot_ref[0]
        at = spot * sets + j
        updated = []
        for c in range(choices):
            total, count = 0.0, 0.0
            for p in range(paths):
                count += jnp.where((flags_ref[p] == 1) & (member_ref[p, at] == c), 1.0, 0.0)
            for q in range(sources):
                p = lead_of(flags_ref, q) if single else q
                weight = jnp.where((flags_ref[p] == 1) & (member_ref[p, at] == c), 1.0, 0.0)
                total = total + weight * shares[q].astype(jnp.float32)
            expert, moved = refreshed(
                total, jnp.maximum(count, 1.0), common_ref[0, c], inertia_ref[0, c]
            )
            expert_out[0, c] = expert
            inertia_out[0, c] = moved
            updated.append(expert.astype(jnp.bfloat16))

        def choose(index):
            chosen = updated[0]
            for c in range(1, choices):
                chosen = jnp.where(index == c, updated[c], chosen)
            return chosen

        returned[0, 0] = choose(member_ref[spot, at])
        if single:
            outs[0][...] = choose(late_of(member_ref, flags_ref, at, spot // 2))
            outs[1][...] = choose(member_ref[spot ^ 1, at])
        else:
            for k in range(1, paths):
                outs[k - 1][...] = choose(member_ref[spot ^ k, at])

    block = pl.BlockSpec((1, choices, units, step), lambda t, *_: (j, 0, 0, t))
    flat = pl.BlockSpec((units, step), lambda t, *_: (0, t))
    own = pl.BlockSpec((1, 1, units, step), lambda t, m, f, spot: (0, spot[0] * sets + j, 0, t))
    arrays = [arrived, common, inertia] + list(partial)
    return local_call(
        body,
        (width // step,),
        [pl.BlockSpec((sources, units, step), lambda t, *_: (0, j, t)), block, block]
        + [ANYWHERE] * len(partial),
        [block, block, own] + [flat] * sends,
        [jax.ShapeDtypeStruct(common.shape, jnp.float32)] * 2
        + [jax.ShapeDtypeStruct(shape, jnp.bfloat16)]
        + [jax.ShapeDtypeStruct((units, width), jnp.bfloat16)] * sends,
        scalars,
        arrays,
        {6 + i: i for i in range(len(partial))},
    )


def place_block(scalars, returned, block, j, sets, k):
    _, _, units, width = returned.shape
    step = divisor(width, 2048)

    def body(member_ref, flags_ref, spot_ref, block_ref, _, out):
        out[0, 0] = block_ref[...]

    return local_call(
        body,
        (width // step,),
        [pl.BlockSpec((units, step), lambda t, *_: (0, t)), ANYWHERE],
        pl.BlockSpec(
            (1, 1, units, step), lambda t, m, f, spot: (0, (spot[0] ^ k) * sets + j, 0, t)
        ),
        jax.ShapeDtypeStruct(returned.shape, jnp.bfloat16),
        scalars,
        [block, returned],
        {4: 0},
    )


def place_far(scalars, returned, late_block, early_block, mine, j, sets, turn):
    _, _, units, width = returned.shape
    step = divisor(width, 2048)

    def serving(spot):
        return (spot % 2) ^ turn

    def place(spot):
        return (2 * (1 - spot // 2) + serving(spot)) * sets + j

    def body(member_ref, flags_ref, spot_ref, late_ref, early_ref, mine_ref, _, out):
        spot = spot_ref[0]
        at = place(spot)
        gain = jnp.where(flags_ref[spot] == 1, GLOBAL_LEARNING * (1.0 + INERTIA_FACTOR), 0.0)
        late = late_of(member_ref, flags_ref, at, 1 - spot // 2)
        quiet = early_ref[0].astype(jnp.float32) - gain * mine_ref[...].astype(jnp.float32)
        out[0, 0] = jnp.where(
            member_ref[spot, at] == late, late_ref[...], quiet.astype(jnp.bfloat16)
        )

    return local_call(
        body,
        (width // step,),
        [
            pl.BlockSpec((units, step), lambda t, *_: (0, t)),
            pl.BlockSpec((1, units, step), lambda t, *_: (j, 0, t)),
            pl.BlockSpec((units, step), lambda t, m, f, spot: (serving(spot[0]) * sets + j, t)),
            ANYWHERE,
        ],
        pl.BlockSpec((1, 1, units, step), lambda t, m, f, spot: (0, place(spot[0]), 0, t)),
        jax.ShapeDtypeStruct(returned.shape, jnp.bfloat16),
        scalars,
        [late_block, early_block, mine, returned],
        {6: 0},
    )


def per_device(
    input_activation_matrix,
    output_sensitivity,
    trajectory_initial_parameters,
    trajectory_gradient_average,
    trajectory_squared_average,
    common_expert_parameters,
    outer_inertia,
    trajectory_membership,
    punctual_flags,
):
    set_count, local_units, row_width = trajectory_initial_parameters.shape[1:]
    rows = set_count * local_units
    path_count = lax.axis_size("path")
    owned_sets = set_count // path_count
    choices = common_expert_parameters.shape[1]
    plan = Plan(
        path_count,
        lax.axis_size("fsdp"),
        input_activation_matrix.shape[1],
        row_width // 2,
        rows,
    )
    x, g = input_activation_matrix[0], output_sensitivity[0]
    r, m, v = (
        array[0].reshape(rows, row_width)
        for array in (
            trajectory_initial_parameters,
            trajectory_gradient_average,
            trajectory_squared_average,
        )
    )
    common, inertia = common_expert_parameters, outer_inertia
    flags = punctual_flags
    scalars = (
        trajectory_membership,
        flags,
        lax.axis_index("path").astype(jnp.int32)[None],
    )
    shape = (1, set_count, local_units, row_width)

    def finish(arrived, alone, j, partial):
        return finish_set(
            scalars, common, inertia, arrived, j, alone, path_count, shape, partial
        )

    def both():
        (arrived,) = run_path(plan, False, flags, x, g, r, m, v)
        hops = list(range(path_count - 1, 0, -1))
        trade = {k: [(p, p ^ k) for p in range(path_count)] for k in hops}
        moved, partial = [], ()
        for j in range(owned_sets):
            *partial, = finish(arrived, False, j, partial)
            blocks, partial = partial[3:], partial[:3]
            moved.append({k: lax.ppermute(blocks[k - 1], "path", trade[k]) for k in hops})
        experts, inertias, returned = partial
        for j in range(owned_sets):
            for k in reversed(hops):
                returned = place_block(scalars, returned, moved[j][k], j, owned_sets, k)
        return experts, inertias, returned

    def single():
        cross = [(p, p ^ 2) for p in range(path_count)]
        swap = [(p, p ^ 1) for p in range(path_count)]
        base = pick_early(scalars, common, inertia)
        early = lax.ppermute(base, "path", cross)
        arrived, mine = run_path(plan, True, flags, x, g, r, m, v)
        still = (early, lax.ppermute(early, "path", swap))
        moved, beside, partial = [], [], ()
        for j in range(owned_sets):
            *partial, late_block, near_block = finish(arrived, True, j, partial)
            sent = lax.ppermute(late_block, "path", cross)
            moved.append((sent, lax.ppermute(sent, "path", swap)))
            beside.append(lax.ppermute(near_block, "path", swap))
        experts, inertias, returned = partial
        for j in range(owned_sets):
            returned = place_block(scalars, returned, beside[j], j, owned_sets, 1)
        for j in range(owned_sets):
            for turn in range(2):
                returned = place_far(
                    scalars, returned, moved[j][turn], still[turn], mine, j, owned_sets, turn
                )
        return experts, inertias, returned

    if path_count == 4 and choices == 2:
        lone = jnp.max(flags.reshape(2, 2).sum(axis=1)) <= 1
        return lax.cond(lone, single, both)
    return both()


def solution(mesh):
    placed = (
        P("path", "fsdp", None),
        P("path", "fsdp", None),
        P("path", None, "fsdp", None),
        P("path", None, "fsdp", None),
        P("path", None, "fsdp", None),
        P("path", None, "fsdp", None),
        P("path", None, "fsdp", None),
        P(),
        P(),
    )
    return jax.shard_map(
        per_device,
        mesh=mesh,
        in_specs=placed,
        out_specs=(
            P("path", None, "fsdp", None),
            P("path", None, "fsdp", None),
            P("path", None, "fsdp", None),
        ),
        check_vma=False,
    )
```

profile of v0, /device:TPU:0, one launch (start us, length us, event | category | flops | bytes accessed | tf_op | source)
XLA Modules:
  0.0 227.9 jit_solution(4147057602409295329)
XLA Ops:
  0.6 0.7 reshape.9
  1.5 0.6 reduce_max.9
  2.8 225.1 %conditional.1 = (f32[2,2,128,4096]{3,2,1,0:T(8,128)}, f32[2,2,128,4096]{3,2,1,0:T(8,128)}, bf16[1,8,128,4096]{3,2,1,0:T(8,128)(2,1)}) conditional(s32[]{:T(128)} %convert_element_type.3, (s32[4]{0:T(128)}, bf16[1,192,2048]{2,1,0:T(8,128)(2,1)}, bf16[1,192,2048]{2,1,0:T(8,128)(2,1)}, bf16[1,8,128,4096]{3,2,1,0:T(8,128)(2,1)}, ...), branch_computations={%region_2.0_spmd, %region_3.0_spmd} | conditional | flops 25935478784 | bytes 273679488 | solution.py:696
  2.8 6.3 %branch_1_fun.11 = bf16[2,128,4096]{2,1,0:T(8,128)(2,1)} custom-call(s32[4,8]{1,0:T(4,128)} %get-tuple-element.117.member_ref, s32[4]{0:T(128)} %get-tuple-element.63.flags_ref, s32[1]{0:T(128)} %bitcast.6.spot_ref, f32[2,2,128,4096]{3,2,1,0:T(8,128)} %get-tuple-element.119.common_ref, f32[2,2,128,4096]{3,2,1,0:T(8,128)} %get-tuple-element.121.inertia_ref), custom_call_target="tpu_custom_call" | custom-call | flops 16777216 | bytes 16777216 | tf_op jit(solution)/shard_map/cond/branch_1_fun/pallas_call | solution.py:454
  9.1 3.0 %collective-permute-start.8 = (bf16[2,128,4096]{2,1,0:T(8,128)(2,1)}, bf16[2,128,4096]{2,1,0:T(8,128)(2,1)}, u32[]{:S(2)}, u32[]{:S(2)}) collective-permute-start(bf16[2,128,4096]{2,1,0:T(8,128)(2,1)} %branch_1_fun.11), channel_id=1, source_target_pairs={{0,16},{8,24},{16,0},{24,8},{1,17},{9,25},{17,1},{25,9},{2,18},{10... | collective-permute-start | bytes 6291464 | tf_op jit(solution)/shard_map/cond/branch_1_fun/ppermute | solution.py:675
  12.1 134.1 %single_path.1 = (bf16[2,256,4096]{2,1,0:T(8,128)(2,1)}, bf16[512,4096]{1,0:T(8,128)(2,1)}) custom-call(s32[4]{0:T(128)S(1)} %copy-done.15, bf16[192,2048]{1,0:T(8,128)(2,1)S(1)} %bitcast.19, bf16[192,2048]{1,0:T(8,128)(2,1)} %bitcast.21, bf16[1024,4096]{1,0:T(8,128)(2,1)} %bitcast.13, bf16[1024,4096]{1,0:T(8,128)(2,1)} %bitcast.15, bf16[1024,4096]{1,0:T(8,128)(2,1)} %bitcast.17), custom_call_target="tpu_custom_call" | custom-call | flops 25769803776 | bytes 33554432 | tf_op jit(solution)/shard_map/cond/branch_1_fun/single_path/pallas_call | solution.py:416
  146.2 9.6 %branch_1_fun.9 = (f32[2,2,128,4096]{3,2,1,0:T(8,128)}, f32[2,2,128,4096]{3,2,1,0:T(8,128)}, bf16[1,8,128,4096]{3,2,1,0:T(8,128)(2,1)}, bf16[128,4096]{1,0:T(8,128)(2,1)}, bf16[128,4096]{1,0:T(8,128)(2,1)}) custom-call(s32[4,8]{1,0:T(4,128)S(1)} %copy-done.13, s32[4]{0:T(128)S(1)} %copy-done.15, s32[1]{0:T(128)} %bitcast.6.spot_ref, ...), custom_call_target="tpu_custom_call" | custom-call | flops 20971520 | bytes 20971520 | tf_op jit(solution)/shard_map/cond/branch_1_fun/pallas_call | solution.py:454
  155.9 2.6 %collective-permute-start.10 = (bf16[128,4096]{1,0:T(8,128)(2,1)}, bf16[128,4096]{1,0:T(8,128)(2,1)S(1)}, u32[]{:S(2)}, u32[]{:S(2)}) collective-permute-start(bf16[128,4096]{1,0:T(8,128)(2,1)} %get-tuple-element.80), channel_id=1, source_target_pairs={{0,16},{8,24},{16,0},{24,8},{1,17},{9,25},{17,1},{25,9},{2,18},{10... | collective-permute-start | bytes 3145736 | tf_op jit(solution)/shard_map/cond/branch_1_fun/ppermute | solution.py:681
  158.5 9.6 %branch_1_fun.10 = (f32[2,2,128,4096]{3,2,1,0:T(8,128)}, f32[2,2,128,4096]{3,2,1,0:T(8,128)}, bf16[1,8,128,4096]{3,2,1,0:T(8,128)(2,1)}, bf16[128,4096]{1,0:T(8,128)(2,1)}, bf16[128,4096]{1,0:T(8,128)(2,1)}) custom-call(s32[4,8]{1,0:T(4,128)S(1)} %copy-done.13, s32[4]{0:T(128)S(1)} %copy-done.15, ...), custom_call_target="tpu_custom_call", output_to_operand_aliasing={{0}: (6, {}), {1}: (7, {}), {2}: (8, {})} | custom-call | flops 46137344 | bytes 46137344 | tf_op jit(solution)/shard_map/cond/branch_1_fun/pallas_call | solution.py:454
  168.1 0.2 collective-permute-start.6
  168.3 0.4 collective-permute-start.13
  168.7 0.1 collective-permute-start.12
  168.8 13.9 %collective-permute-done.10.late_ref = bf16[128,4096]{1,0:T(8,128)(2,1)S(1)} collective-permute-done((bf16[128,4096]{1,0:T(8,128)(2,1)}, bf16[128,4096]{1,0:T(8,128)(2,1)S(1)}, u32[]{:S(2)}, u32[]{:S(2)}) %collective-permute-start.10) | collective-permute-done | bytes 1048608 | tf_op jit(solution)/shard_map/cond/branch_1_fun/ppermute | solution.py:681
  182.7 21.9 %collective-permute-done.6.late_ref = bf16[128,4096]{1,0:T(8,128)(2,1)S(1)} collective-permute-done((bf16[128,4096]{1,0:T(8,128)(2,1)}, bf16[128,4096]{1,0:T(8,128)(2,1)S(1)}, u32[]{:S(2)}, u32[]{:S(2)}) %collective-permute-start.6) | collective-permute-done | bytes 1048608 | tf_op jit(solution)/shard_map/cond/branch_1_fun/ppermute | solution.py:681
  204.6 2.6 %branch_1_fun.12._ = bf16[1,8,128,4096]{3,2,1,0:T(8,128)(2,1)} custom-call(s32[4,8]{1,0:T(4,128)S(1)} %copy-done.13, s32[4]{0:T(128)S(1)} %copy-done.15, s32[1]{0:T(128)} %bitcast.6.spot_ref, bf16[128,4096]{1,0:T(8,128)(2,1)} %collective-permute-done.13.block_ref, bf16[1,8,128,4096]{3,2,1,0:T(8,128)(2,1)} %get-tuple-element.83._), custom_call_target="tpu_custom_call", output_to_operand_aliasing={{}: (4, {})} | custom-call | flops 9437184 | bytes 9437184 | tf_op jit(solution)/shard_map/cond/branch_1_fun/pallas_call | solution.py:454
  207.2 1.0 copy-done.11
  208.2 2.6 %branch_1_fun.13._ = bf16[1,8,128,4096]{3,2,1,0:T(8,128)(2,1)} custom-call(s32[4,8]{1,0:T(4,128)S(1)} %copy-done.13, s32[4]{0:T(128)S(1)} %copy-done.15, s32[1]{0:T(128)} %bitcast.6.spot_ref, bf16[128,4096]{1,0:T(8,128)(2,1)} %copy-done.11, bf16[1,8,128,4096]{3,2,1,0:T(8,128)(2,1)} %branch_1_fun.12._), custom_call_target="tpu_custom_call", output_to_operand_aliasing={{}: (4, {})} | custom-call | flops 9437184 | bytes 9437184 | tf_op jit(solution)/shard_map/cond/branch_1_fun/pallas_call | solution.py:454
  210.9 3.4 %branch_1_fun.14._ = bf16[1,8,128,4096]{3,2,1,0:T(8,128)(2,1)} custom-call(s32[4,8]{1,0:T(4,128)S(1)} %copy-done.13, s32[4]{0:T(128)S(1)} %copy-done.15, s32[1]{0:T(128)} %bitcast.6.spot_ref, bf16[128,4096]{1,0:T(8,128)(2,1)} %copy-done.1, bf16[2,128,4096]{2,1,0:T(8,128)(2,1)} %collective-permute-done.8.early_ref, ...), custom_call_target="tpu_custom_call", output_to_operand_aliasing={{}: (6, {})} | custom-call | flops 15728640 | bytes 15728640 | tf_op jit(solution)/shard_map/cond/branch_1_fun/pallas_call | solution.py:454
  214.3 1.1 copy-done.10
  215.3 1.4 copy-done
  216.7 3.4 %branch_1_fun.15._ = bf16[1,8,128,4096]{3,2,1,0:T(8,128)(2,1)} custom-call(s32[4,8]{1,0:T(4,128)S(1)} %copy-done.13, s32[4]{0:T(128)S(1)} %copy-done.15, s32[1]{0:T(128)} %bitcast.6.spot_ref, bf16[128,4096]{1,0:T(8,128)(2,1)} %copy-done.10, bf16[2,128,4096]{2,1,0:T(8,128)(2,1)} %copy-done, ...), custom_call_target="tpu_custom_call", output_to_operand_aliasing={{}: (6, {})} | custom-call | flops 15728640 | bytes 15728640 | tf_op jit(solution)/shard_map/cond/branch_1_fun/pallas_call | solution.py:454
  220.1 3.4 %branch_1_fun.16._ = bf16[1,8,128,4096]{3,2,1,0:T(8,128)(2,1)} custom-call(s32[4,8]{1,0:T(4,128)S(1)} %copy-done.13, s32[4]{0:T(128)S(1)} %copy-done.15, s32[1]{0:T(128)} %bitcast.6.spot_ref, bf16[128,4096]{1,0:T(8,128)(2,1)} %copy-done.2, bf16[2,128,4096]{2,1,0:T(8,128)(2,1)} %collective-permute-done.8.early_ref, ...), custom_call_target="tpu_custom_call", output_to_operand_aliasing={{}: (6, {})} | custom-call | flops 15728640 | bytes 15728640 | tf_op jit(solution)/shard_map/cond/branch_1_fun/pallas_call | solution.py:454
  223.5 1.0 copy-done.7
  224.5 3.4 %branch_1_fun.17 = bf16[1,8,128,4096]{3,2,1,0:T(8,128)(2,1)} custom-call(s32[4,8]{1,0:T(4,128)S(1)} %copy-done.13, s32[4]{0:T(128)S(1)} %copy-done.15, s32[1]{0:T(128)} %bitcast.6.spot_ref, bf16[128,4096]{1,0:T(8,128)(2,1)} %copy-done.7, bf16[2,128,4096]{2,1,0:T(8,128)(2,1)} %copy-done, ...), custom_call_target="tpu_custom_call", output_to_operand_aliasing={{}: (6, {})} | custom-call | flops 15728640 | bytes 15728640 | tf_op jit(solution)/shard_map/cond/branch_1_fun/pallas_call | solution.py:454
  (24 shorter events, 0.2 us)
Async XLA Ops:
  2.8 9.3 %copy-start.15 = (s32[4]{0:T(128)S(1)}, s32[4]{0:T(128)}, u32[]{:S(2)}) copy-start(s32[4]{0:T(128)} %get-tuple-element.63.flags_ref) | copy-start | bytes 52 | tf_op jit(solution)/shard_map/cond
  2.8 9.3 %copy-start.16 = (bf16[1,192,2048]{2,1,0:T(8,128)(2,1)S(1)}, bf16[1,192,2048]{2,1,0:T(8,128)(2,1)}, u32[]{:S(2)}) copy-start(bf16[1,192,2048]{2,1,0:T(8,128)(2,1)} %get-tuple-element.123) | copy-start | bytes 2359300 | tf_op jit(solution)/shard_map/cond
  9.1 149.4 %collective-permute-start.8 = (bf16[2,128,4096]{2,1,0:T(8,128)(2,1)}, bf16[2,128,4096]{2,1,0:T(8,128)(2,1)}, u32[]{:S(2)}, u32[]{:S(2)}) collective-permute-start(bf16[2,128,4096]{2,1,0:T(8,128)(2,1)} %branch_1_fun.11), channel_id=1, source_target_pairs={{0,16},{8,24},{16,0},{24,8},{1,17},{9,25},{17,1},{25,9},{2,18},{10... | collective-permute-start | bytes 6291464 | tf_op jit(solution)/shard_map/cond/branch_1_fun/ppermute | solution.py:675
  12.1 134.1 %copy-start.13 = (s32[4,8]{1,0:T(4,128)S(1)}, s32[4,8]{1,0:T(4,128)}, u32[]{:S(2)}) copy-start(s32[4,8]{1,0:T(4,128)} %get-tuple-element.117.member_ref) | copy-start | bytes 388 | tf_op jit(solution)/shard_map/cond
  155.9 26.8 %collective-permute-start.10 = (bf16[128,4096]{1,0:T(8,128)(2,1)}, bf16[128,4096]{1,0:T(8,128)(2,1)S(1)}, u32[]{:S(2)}, u32[]{:S(2)}) collective-permute-start(bf16[128,4096]{1,0:T(8,128)(2,1)} %get-tuple-element.80), channel_id=1, source_target_pairs={{0,16},{8,24},{16,0},{24,8},{1,17},{9,25},{17,1},{25,9},{2,18},{10... | collective-permute-start | bytes 3145736 | tf_op jit(solution)/shard_map/cond/branch_1_fun/ppermute | solution.py:681
  158.5 55.8 %collective-permute-start.9 = (bf16[2,128,4096]{2,1,0:T(8,128)(2,1)}, bf16[2,128,4096]{2,1,0:T(8,128)(2,1)S(1)}, u32[]{:S(2)}, u32[]{:S(2)}) collective-permute-start(bf16[2,128,4096]{2,1,0:T(8,128)(2,1)} %collective-permute-done.8.early_ref), channel_id=1, source_target_pairs={{0,8},{8,0},{16,24},{24,16},{1,9},{9,1},{17,25},{25,17},{2,10},{10... | collective-permute-start | bytes 6291464 | tf_op jit(solution)/shard_map/cond/branch_1_fun/ppermute | solution.py:677
  168.1 36.5 %collective-permute-start.6 = (bf16[128,4096]{1,0:T(8,128)(2,1)}, bf16[128,4096]{1,0:T(8,128)(2,1)S(1)}, u32[]{:S(2)}, u32[]{:S(2)}) collective-permute-start(bf16[128,4096]{1,0:T(8,128)(2,1)} %get-tuple-element.78), channel_id=1, source_target_pairs={{0,16},{8,24},{16,0},{24,8},{1,17},{9,25},{17,1},{25,9},{2,18},{10... | collective-permute-start | bytes 3145736 | tf_op jit(solution)/shard_map/cond/branch_1_fun/ppermute | solution.py:681
  168.3 36.3 %collective-permute-start.13 = (bf16[128,4096]{1,0:T(8,128)(2,1)}, bf16[128,4096]{1,0:T(8,128)(2,1)}, u32[]{:S(2)}, u32[]{:S(2)}) collective-permute-start(bf16[128,4096]{1,0:T(8,128)(2,1)} %get-tuple-element.82), channel_id=1, source_target_pairs={{0,8},{8,0},{16,24},{24,16},{1,9},{9,1},{17,25},{25,17},{2,10},{10... | collective-permute-start | bytes 3145736 | tf_op jit(solution)/shard_map/cond/branch_1_fun/ppermute | solution.py:683
  168.7 38.5 %collective-permute-start.12 = (bf16[128,4096]{1,0:T(8,128)(2,1)}, bf16[128,4096]{1,0:T(8,128)(2,1)S(1)}, u32[]{:S(2)}, u32[]{:S(2)}) collective-permute-start(bf16[128,4096]{1,0:T(8,128)(2,1)} %get-tuple-element.81), channel_id=1, source_target_pairs={{0,8},{8,0},{16,24},{24,16},{1,9},{9,1},{17,25},{25,17},{2,10},{10... | collective-permute-start | bytes 3145736 | tf_op jit(solution)/shard_map/cond/branch_1_fun/ppermute | solution.py:683
  182.7 24.5 %copy-start.1 = (bf16[128,4096]{1,0:T(8,128)(2,1)}, bf16[128,4096]{1,0:T(8,128)(2,1)S(1)}, u32[]{:S(2)}) copy-start(bf16[128,4096]{1,0:T(8,128)(2,1)S(1)} %collective-permute-done.10.late_ref) | copy-start | bytes 3145732 | tf_op jit(solution)/shard_map/cond
  182.7 31.6 %collective-permute-start.11 = (bf16[128,4096]{1,0:T(8,128)(2,1)S(1)}, bf16[128,4096]{1,0:T(8,128)(2,1)S(1)}, u32[]{:S(2)}, u32[]{:S(2)}) collective-permute-start(bf16[128,4096]{1,0:T(8,128)(2,1)S(1)} %collective-permute-done.10.late_ref), channel_id=1, source_target_pairs={{0,8},{8,0},{16,24},{24,16},{1,9},{9,1},{17,25},{25,17},{2,10},{10... | collective-permute-start | bytes 3145736 | tf_op jit(solution)/shard_map/cond/branch_1_fun/ppermute | solution.py:682
  204.6 2.6 %copy-start.2 = (bf16[128,4096]{1,0:T(8,128)(2,1)}, bf16[128,4096]{1,0:T(8,128)(2,1)S(1)}, u32[]{:S(2)}) copy-start(bf16[128,4096]{1,0:T(8,128)(2,1)S(1)} %collective-permute-done.6.late_ref) | copy-start | bytes 3145732 | tf_op jit(solution)/shard_map/cond
  204.6 18.9 %collective-permute-start.7 = (bf16[128,4096]{1,0:T(8,128)(2,1)S(1)}, bf16[128,4096]{1,0:T(8,128)(2,1)S(1)}, u32[]{:S(2)}, u32[]{:S(2)}) collective-permute-start(bf16[128,4096]{1,0:T(8,128)(2,1)S(1)} %collective-permute-done.6.late_ref), channel_id=1, source_target_pairs={{0,8},{8,0},{16,24},{24,16},{1,9},{9,1},{17,25},{25,17},{2,10},{10... | collective-permute-start | bytes 3145736 | tf_op jit(solution)/shard_map/cond/branch_1_fun/ppermute | solution.py:682
  207.2 1.0 copy-start.11
  214.3 1.1 copy-start.10
  215.3 1.4 copy-start
  223.5 1.0 copy-start.7
where the time goes:
time: 228 us
  Pallas kernels  178 us (78%)
  waiting for transfers between devices  35.8 us (16%)
  starting transfers between devices  6.28 us (3%)
  local copies, waits for them, and re-layouts  5.18 us (2%)
    pallas_call x1, Pallas kernels, run_path(): pl.pallas_call(body, out_shape=shapes, in_specs=[pl.BlockSpec(memory_spac...  134 us
    pallas_call x9, Pallas kernels, local_call(): pl.pallas_call(body, grid_spec=pltpu.PrefetchScalarGridSpec(num_scalar_pr...  44.4 us
    ppermute x2, waiting for transfers between devices, single(): sent = lax.ppermute(late_block, 'path', cross)  35.8 us
  transfers between devices with their start and end apart: 8, of which 2 were waited for; matrix products, arithmetic and copies ran while one was open for 0% of the time, Pallas kernels for 74%

commit v1 on v0

--- a/solution.py
+++ b/solution.py
@@ -33,6 +33,21 @@
     second_new = BETA_TWO * second.astype(jnp.float32) + (1.0 - BETA_TWO) * grads * grads
     direction = first_new / corr_one / (jnp.sqrt(second_new / corr_two) + ADAM_EPS)
     return (INNER_RATE * (direction + DECAY * start.astype(jnp.float32))).astype(jnp.bfloat16)
+
+
+def adam_folded(product, scale, first, second, start):
+    corr_one = 1.0 - BETA_ONE**STEP
+    corr_two = 1.0 - BETA_TWO**STEP
+    up = (BETA_ONE / corr_one) * first.astype(jnp.float32) + (
+        (1.0 - BETA_ONE) / corr_one * scale
+    ) * product
+    spread = (BETA_TWO / corr_two) * second.astype(jnp.float32) + (
+        (1.0 - BETA_TWO) / corr_two * scale * scale
+    ) * (product * product)
+    down = spread * lax.rsqrt(spread) + ADAM_EPS
+    return (
+        INNER_RATE * (up / down) + (INNER_RATE * DECAY) * start.astype(jnp.float32)
+    ).astype(jnp.bfloat16)
 
 
 def gelu_pair(pre):
@@ -64,6 +79,9 @@
         self.tile = divisor(features, 512)
         self.tiles = self.width // self.tile
         self.units = divisor(rows, 256)
+        self.pieces = 2 if self.half % 32 == 0 else 1
+        self.slots = 3
+        self.chunk = 256 if self.tokens % 256 == 0 else self.tokens
 
 
 def ring_neighbours(index, size):
@@ -431,6 +449,373 @@
     )(flags, x, g, r, m, v)
 
 
+def survivor_kernel(
+    plan, rounds, flags_ref, x_hbm, g_hbm, r_hbm, m_hbm, v_hbm, arr_hbm, own_hbm, *scratch
+):
+    (xg, params, hidden, first, second, pseudo, raw, swapped) = scratch[:8]
+    (cross_in, own_in, cross_out, own_out) = scratch[8:12]
+    (load_sem, moment_sem, send_sem, recv_sem, side_send, side_recv, out_send, out_recv, keep_sem) = (
+        scratch[12:]
+    )
+    n, shard, half = plan.ring, plan.shard, plan.half
+    features, owned, tile, tiles = plan.features, plan.owned, plan.tile, plan.tiles
+    pieces, slots = plan.pieces, plan.slots
+    path = lax.axis_index("path")
+    place = lax.axis_index("fsdp")
+    ahead, behind = ring_neighbours(place, n)
+    core, chip = path % 2, path // 2
+    sibling = path + 1 - 2 * core
+    far = (1 - chip) * 2
+    leading = jnp.where(lead_of(flags_ref, chip) == path, 1, 0)
+
+    barrier = pltpu.get_barrier_semaphore()
+    partners = [(path, ahead), (path, behind), (sibling, place), (far + core, place)]
+    for to_path, to_place in partners:
+        pl.semaphore_signal(
+            barrier, inc=1, device_id={"path": to_path, "fsdp": to_place}, device_id_type=MESH
+        )
+
+    def cols_of(t):
+        return pl.ds(pl.multiple_of(t * tile, tile), tile)
+
+    def rows_of(p):
+        return pl.ds(pl.multiple_of(p * owned, owned), owned)
+
+    def moments(index):
+        cols, slot = cols_of(index % tiles), index % 2
+        return (
+            pltpu.make_async_copy(m_hbm.at[:, cols], first.at[slot], moment_sem.at[0, slot]),
+            pltpu.make_async_copy(v_hbm.at[:, cols], second.at[slot], moment_sem.at[1, slot]),
+        )
+
+    loads = (
+        pltpu.make_async_copy(x_hbm, raw.at[0], load_sem.at[0]),
+        pltpu.make_async_copy(g_hbm, raw.at[1], load_sem.at[1]),
+    )
+    for load in loads:
+        load.start()
+    load_params = pltpu.make_async_copy(r_hbm, params, load_sem.at[2])
+    load_params.start()
+    for load in moments(0):
+        load.start()
+    pl.semaphore_wait(barrier, len(partners))
+    for load in loads:
+        load.wait()
+    swap = pltpu.make_async_remote_copy(
+        src_ref=raw.at[1 - core],
+        dst_ref=swapped,
+        send_sem=load_sem.at[3],
+        recv_sem=load_sem.at[4],
+        device_id={"path": sibling, "fsdp": place},
+        device_id_type=MESH,
+    )
+    swap.start()
+    swap.wait()
+    for turn in range(rounds):
+        mine = leading == 1 - turn
+        xg[turn, core, 0:shard] = jnp.where(mine, raw[core], swapped[...])
+
+    def ring_copies(turn, step):
+        copies = []
+        for piece in range(pieces):
+            for way in range(2):
+                size = half // pieces
+                at = way * half + piece * size
+                source = pl.ds(pl.multiple_of((step - 1) * shard + at, 16), size)
+                target = pl.ds(pl.multiple_of(step * shard + at, 16), size)
+                copies.append(
+                    pltpu.make_async_remote_copy(
+                        src_ref=xg.at[turn, core, source],
+                        dst_ref=xg.at[turn, core, target],
+                        send_sem=send_sem.at[turn, way * pieces + piece, step],
+                        recv_sem=recv_sem.at[turn, way * pieces + piece, step],
+                        device_id={"path": path, "fsdp": behind if way else ahead},
+                        device_id_type=MESH,
+                    )
+                )
+        return copies
+
+    def side_copy(turn, slot, array):
+        rows = pl.ds(pl.multiple_of(slot * shard, shard), shard)
+        return pltpu.make_async_remote_copy(
+            src_ref=xg.at[turn, array, rows],
+            dst_ref=xg.at[turn, array, rows],
+            send_sem=side_send.at[turn, slot],
+            recv_sem=side_recv.at[turn, slot],
+            device_id={"path": sibling, "fsdp": place},
+            device_id_type=MESH,
+        )
+
+    def begin(turn):
+        for copy in ring_copies(turn, 1):
+            copy.start()
+        side_copy(turn, 0, core).start()
+
+    begin(0)
+    load_params.wait()
+
+    def forward(turn, j):
+        rows = pl.ds(pl.multiple_of(j * plan.chunk, plan.chunk), plan.chunk)
+
+        def unit(u, carry):
+            strip = pl.ds(pl.multiple_of(u * plan.units, plan.units), plan.units)
+            nt = (((1,), (1,)), ((), ()))
+            pre = lax.dot_general(
+                params[strip, 0:features], xg[turn, 0, rows], nt, preferred_element_type=jnp.float32
+            ) * (features**-0.5)
+            act, slope = gelu_pair(pre)
+            hidden[1, strip, rows] = act.astype(jnp.bfloat16)
+            back = lax.dot_general(
+                params[strip, features : 2 * features],
+                xg[turn, 1, rows],
+                nt,
+                preferred_element_type=jnp.float32,
+            ) * ((SETS * UNIT) ** -0.5)
+            hidden[0, strip, rows] = (back * slope).astype(jnp.bfloat16)
+            return carry
+
+        lax.fori_loop(0, plan.rows // plan.units, unit, 0)
+
+    def share_copy(index, which):
+        owner = (far + 1 - core) if which == 0 else sibling
+        return pltpu.make_async_remote_copy(
+            src_ref=pseudo.at[index % slots, rows_of(owner)],
+            dst_ref=(cross_in if which == 0 else own_in).at[index],
+            send_sem=out_send.at[index, which],
+            recv_sem=out_recv.at[index, which],
+            device_id={"path": sibling, "fsdp": place},
+            device_id_type=MESH,
+        )
+
+    def cross_copy(index):
+        return pltpu.make_async_remote_copy(
+            src_ref=cross_out.at[index % tiles],
+            dst_ref=arr_hbm.at[index // tiles * 2 + chip, :, cols_of(index % tiles)],
+            send_sem=out_send.at[index, 2],
+            recv_sem=out_recv.at[index, 2],
+            device_id={"path": far + core, "fsdp": place},
+            device_id_type=MESH,
+        )
+
+    def near_copy(index):
+        return pltpu.make_async_copy(
+            own_out.at[index % tiles],
+            arr_hbm.at[index // tiles * 2 + chip, :, cols_of(index % tiles)],
+            keep_sem.at[0, index],
+        )
+
+    def own_copy(index):
+        rows = pl.ds(pl.multiple_of(far * owned, 2 * owned), 2 * owned)
+        out = pl.ds(pl.multiple_of(index // tiles * 2 * owned, 2 * owned), 2 * owned)
+        return pltpu.make_async_copy(
+            pseudo.at[index % slots, rows],
+            own_hbm.at[out, cols_of(index % tiles)],
+            keep_sem.at[1, index],
+        )
+
+    def pick(index):
+        mine = leading == 1 - index // tiles
+
+        @pl.when(index >= tiles)
+        def _():
+            cross_copy(index - tiles).wait_send()
+            near_copy(index - tiles).wait()
+
+        slot, t = index % slots, index % tiles
+        share_copy(index, 0).wait_recv()
+        cross_out[t] = jnp.where(mine, pseudo[slot, rows_of(far + core)], cross_in[index])
+        cross_copy(index).start()
+        share_copy(index, 1).wait_recv()
+        own_out[t] = jnp.where(mine, pseudo[slot, rows_of(path)], own_in[index])
+        near_copy(index).start()
+
+    def release(index):
+        share_copy(index, 0).wait_send()
+        share_copy(index, 1).wait_send()
+        own_copy(index).wait()
+
+    def grad_tile(index, carry):
+        moment, slot = index % 2, index % slots
+        turn, t = index // tiles, index % tiles
+
+        @pl.when(index + 1 < rounds * tiles)
+        def _():
+            for load in moments(index + 1):
+                load.start()
+
+        @pl.when(index >= slots)
+        def _():
+            release(index - slots)
+
+        for load in moments(index):
+            load.wait()
+        side = t // (tiles // 2)
+        scale = jnp.where(side == 0, features**-0.5, (SETS * UNIT) ** -0.5).astype(jnp.float32)
+        token_cols = pl.ds(pl.multiple_of(t % (tiles // 2) * tile, tile), tile)
+
+        def unit(u, inner):
+            strip = pl.ds(pl.multiple_of(u * plan.units, plan.units), plan.units)
+            product = jnp.dot(
+                hidden[side, strip, :],
+                xg[turn, side, :, token_cols],
+                preferred_element_type=jnp.float32,
+            )
+            pseudo[slot, strip, :] = adam_folded(
+                product,
+                scale,
+                first[moment, strip, :],
+                second[moment, strip, :],
+                params[strip, cols_of(t)],
+            )
+            return inner
+
+        lax.fori_loop(0, plan.rows // plan.units, unit, 0)
+        share_copy(index, 0).start()
+        share_copy(index, 1).start()
+        own_copy(index).start()
+
+        @pl.when(index > 0)
+        def _():
+            pick(index - 1)
+
+        return carry
+
+    spread = -(-tiles // 4)
+    last = rounds * n
+
+    def stage(i, carry):
+        turn, k = i // n, i % n
+
+        @pl.when((k > 0) & (i < last))
+        def _():
+            arrivals = ring_copies(turn, k)
+
+            @pl.when(k < n - 1)
+            def _():
+                for here, onward in zip(arrivals, ring_copies(turn, k + 1)):
+                    here.wait_recv()
+                    onward.start()
+
+            @pl.when(k == n - 1)
+            def _():
+                for here in arrivals:
+                    here.wait_recv()
+
+            side_copy(turn, k, core).start()
+
+        if rounds > 1:
+
+            @pl.when((k == n - 1) & (turn + 1 < rounds))
+            def _():
+                begin(turn + 1)
+
+        @pl.when(i < last)
+        def _():
+            side_copy(turn, k, 1 - core).wait_recv()
+
+        begun, ended = k * shard // plan.chunk, (k + 1) * shard // plan.chunk
+        if rounds == 1:
+            low = jnp.where(i == last, 0, tiles)
+            high = tiles
+        else:
+            held = (turn == 1) & (k < 4)
+            low = jnp.where(held, k * spread, jnp.where(i == last, tiles, 0))
+            high = jnp.where(
+                held, jnp.minimum(k * spread + spread, tiles), jnp.where(i == last, 2 * tiles, 0)
+            )
+            begun = jnp.where((turn == 1) & (k < 6), jnp.where(k == 5, 2, 0), begun)
+            ended = jnp.where((turn == 1) & (k < 5), jnp.where(k == 4, 2, 0), ended)
+        lax.fori_loop(low, high, grad_tile, 0)
+
+        def ready(j, inner):
+            forward(turn, j)
+            return inner
+
+        lax.fori_loop(jnp.where(i < last, begun, ended), ended, ready, 0)
+        return carry
+
+    lax.fori_loop(0, last + 1, stage, 0)
+    pick(rounds * tiles - 1)
+
+    def drain_ring(i, carry):
+        turn, k = i // n, i % n
+        side_copy(turn, k, core).wait_send()
+
+        @pl.when(k > 0)
+        def _():
+            for copy in ring_copies(turn, k):
+                copy.wait_send()
+
+        return carry
+
+    lax.fori_loop(0, rounds * n, drain_ring, 0)
+
+    def drain(index, carry):
+        @pl.when(index >= rounds * tiles - slots)
+        def _():
+            release(index)
+
+        @pl.when(index >= (rounds - 1) * tiles)
+        def _():
+            near_copy(index).wait()
+            cross_copy(index).wait_send()
+
+        cross_copy(index).wait_recv()
+        return carry
+
+    lax.fori_loop(0, rounds * tiles, drain, 0)
+
+
+def run_survivors(plan, rounds, flags, x, g, r, m, v):
+    bf16, dma = jnp.bfloat16, pltpu.SemaphoreType.DMA
+    width, tile, tiles = plan.width, plan.tile, plan.tiles
+    served = pltpu.VMEM((rounds * tiles, plan.owned, tile), bf16)
+    sent = pltpu.VMEM((tiles, plan.owned, tile), bf16)
+    scratch = [
+        pltpu.VMEM((rounds, 2, plan.tokens, plan.features), bf16),
+        pltpu.VMEM((plan.rows, width), bf16),
+        pltpu.VMEM((2, plan.rows, plan.tokens), bf16),
+        pltpu.VMEM((2, plan.rows, tile), bf16),
+        pltpu.VMEM((2, plan.rows, tile), bf16),
+        pltpu.VMEM((plan.slots, plan.rows, tile), bf16),
+        pltpu.VMEM((2, plan.shard, plan.features), bf16),
+        pltpu.VMEM((plan.shard, plan.features), bf16),
+        served,
+        served,
+        sent,
+        sent,
+        dma((5,)),
+        dma((2, 2)),
+        dma((rounds, 2 * plan.pieces, plan.ring)),
+        dma((rounds, 2 * plan.pieces, plan.ring)),
+        dma((rounds, plan.ring)),
+        dma((rounds, plan.ring)),
+        dma((rounds * tiles, 3)),
+        dma((rounds * tiles, 3)),
+        dma((2, rounds * tiles)),
+    ]
+    anywhere = pl.BlockSpec(memory_space=pl.ANY)
+    return pl.pallas_call(
+        functools.partial(survivor_kernel, plan, rounds),
+        out_shape=[
+            jax.ShapeDtypeStruct((2 * rounds, plan.owned, width), bf16),
+            jax.ShapeDtypeStruct((2 * rounds * plan.owned, width), bf16),
+        ],
+        in_specs=[pl.BlockSpec(memory_space=pltpu.SMEM)] + [anywhere] * 5,
+        out_specs=[anywhere] * 2,
+        scratch_shapes=scratch,
+        compiler_params=pltpu.CompilerParams(
+            collective_id=rounds, has_side_effects=True, vmem_limit_bytes=67043328
+        ),
+        cost_estimate=pl.CostEstimate(
+            flops=8 * plan.tokens * plan.features * plan.rows * rounds,
+            bytes_accessed=8 * plan.rows * width,
+            transcendentals=0,
+        ),
+        name="survivors",
+    )(flags, x, g, r, m, v)
+
+
 def refreshed(total, tally, common, inertia):
     average = total / tally
     inertia = INERTIA_FACTOR * inertia + average
@@ -490,11 +875,11 @@
     )
 
 
-def finish_set(scalars, common, inertia, arrived, j, single, paths, shape, partial):
+def finish_set(scalars, common, inertia, arrived, j, rounds, paths, shape, partial):
     sets, choices, units, width = common.shape
     sources = arrived.shape[0]
-    step = divisor(width, 1024)
-    sends = 2 if single else paths - 1
+    step = divisor(width, 2048)
+    sends = 1 + rounds if rounds else paths - 1
 
     def body(member_ref, flags_ref, spot_ref, shares, common_ref, inertia_ref, *refs):
         expert_out, inertia_out, returned, *outs = refs[-3 - sends :]
@@ -506,7 +891,10 @@
             for p in range(paths):
                 count += jnp.where((flags_ref[p] == 1) & (member_ref[p, at] == c), 1.0, 0.0)
             for q in range(sources):
-                p = lead_of(flags_ref, q) if single else q
+                p = q
+                if rounds:
+                    lead = lead_of(flags_ref, q % 2)
+                    p = lead if q < 2 else 4 * (q % 2) + 1 - lead
                 weight = jnp.where((flags_ref[p] == 1) & (member_ref[p, at] == c), 1.0, 0.0)
                 total = total + weight * shares[q].astype(jnp.float32)
             expert, moved = refreshed(
@@ -523,9 +911,12 @@
             return chosen
 
         returned[0, 0] = choose(member_ref[spot, at])
-        if single:
-            outs[0][...] = choose(late_of(member_ref, flags_ref, at, spot // 2))
+        if rounds:
+            late = late_of(member_ref, flags_ref, at, spot // 2)
+            outs[0][...] = choose(late)
             outs[1][...] = choose(member_ref[spot ^ 1, at])
+            if rounds > 1:
+                outs[2][...] = choose(1 - late)
         else:
             for k in range(1, paths):
                 outs[k - 1][...] = choose(member_ref[spot ^ k, at])
@@ -570,7 +961,14 @@
     )
 
 
-def place_far(scalars, returned, late_block, early_block, mine, j, sets, turn):
+def needs_other(member, flags, at, owner_chip):
+    near, far = 2 * owner_chip, 2 * (1 - owner_chip)
+    changed = (flags[near] == 1) & (flags[near + 1] == 1)
+    changed &= member[near, at] != member[near + 1, at]
+    return changed & (member[far, at] != member[far + 1, at])
+
+
+def place_far(scalars, returned, late_block, early_block, mine, other_block, j, sets, turn):
     _, _, units, width = returned.shape
     step = divisor(width, 2048)
 
@@ -580,30 +978,44 @@
     def place(spot):
         return (2 * (1 - spot // 2) + serving(spot)) * sets + j
 
-    def body(member_ref, flags_ref, spot_ref, late_ref, early_ref, mine_ref, _, out):
+    def body(member_ref, flags_ref, spot_ref, late_ref, early_ref, mine_ref, *refs):
+        out = refs[-1]
         spot = spot_ref[0]
         at = place(spot)
         gain = jnp.where(flags_ref[spot] == 1, GLOBAL_LEARNING * (1.0 + INERTIA_FACTOR), 0.0)
         late = late_of(member_ref, flags_ref, at, 1 - spot // 2)
         quiet = early_ref[0].astype(jnp.float32) - gain * mine_ref[...].astype(jnp.float32)
-        out[0, 0] = jnp.where(
-            member_ref[spot, at] == late, late_ref[...], quiet.astype(jnp.bfloat16)
-        )
-
+        quiet = quiet.astype(jnp.bfloat16)
+        if other_block is not None:
+            sent = needs_other(member_ref, flags_ref, at, 1 - spot // 2)
+            quiet = jnp.where(sent, refs[0][...], quiet)
+        out[0, 0] = jnp.where(member_ref[spot, at] == late, late_ref[...], quiet)
+
+    def mine_at(t, m, flags_ref, spot_ref):
+        spot = spot_ref[0]
+        behind = jnp.where(lead_of(flags_ref, spot // 2) == spot, 0, 1)
+        turn_row = behind * (mine.shape[0] // units - 2 * sets)
+        return (turn_row + serving(spot) * sets + j, t)
+
+    flat = pl.BlockSpec((units, step), lambda t, *_: (0, t))
+    arrays = [late_block, early_block, mine]
+    specs = [
+        flat,
+        pl.BlockSpec((1, units, step), lambda t, *_: (j, 0, t)),
+        pl.BlockSpec((units, step), mine_at),
+    ]
+    if other_block is not None:
+        arrays.append(other_block)
+        specs.append(flat)
     return local_call(
         body,
         (width // step,),
-        [
-            pl.BlockSpec((units, step), lambda t, *_: (0, t)),
-            pl.BlockSpec((1, units, step), lambda t, *_: (j, 0, t)),
-            pl.BlockSpec((units, step), lambda t, m, f, spot: (serving(spot[0]) * sets + j, t)),
-            ANYWHERE,
-        ],
+        specs + [ANYWHERE],
         pl.BlockSpec((1, 1, units, step), lambda t, m, f, spot: (0, place(spot[0]), 0, t)),
         jax.ShapeDtypeStruct(returned.shape, jnp.bfloat16),
         scalars,
-        [late_block, early_block, mine, returned],
-        {6: 0},
+        arrays + [returned],
+        {3 + len(arrays): 0},
     )
 
 
@@ -648,9 +1060,9 @@
     )
     shape = (1, set_count, local_units, row_width)
 
-    def finish(arrived, alone, j, partial):
+    def finish(arrived, rounds, j, partial):
         return finish_set(
-            scalars, common, inertia, arrived, j, alone, path_count, shape, partial
+            scalars, common, inertia, arrived, j, rounds, path_count, shape, partial
         )
 
     def both():
@@ -659,7 +1071,7 @@
         trade = {k: [(p, p ^ k) for p in range(path_count)] for k in hops}
         moved, partial = [], ()
         for j in range(owned_sets):
-            *partial, = finish(arrived, False, j, partial)
+            *partial, = finish(arrived, 0, j, partial)
             blocks, partial = partial[3:], partial[:3]
             moved.append({k: lax.ppermute(blocks[k - 1], "path", trade[k]) for k in hops})
         experts, inertias, returned = partial
@@ -668,32 +1080,77 @@
                 returned = place_block(scalars, returned, moved[j][k], j, owned_sets, k)
         return experts, inertias, returned
 
-    def single():
-        cross = [(p, p ^ 2) for p in range(path_count)]
-        swap = [(p, p ^ 1) for p in range(path_count)]
-        base = pick_early(scalars, common, inertia)
-        early = lax.ppermute(base, "path", cross)
-        arrived, mine = run_path(plan, True, flags, x, g, r, m, v)
+    cross = [(p, p ^ 2) for p in range(path_count)]
+    swap = [(p, p ^ 1) for p in range(path_count)]
+
+    def exchange(rounds, others, arrived, mine, early, needed):
         still = (early, lax.ppermute(early, "path", swap))
-        moved, beside, partial = [], [], ()
+        moved, beside, rest, partial = [], [], [], ()
         for j in range(owned_sets):
-            *partial, late_block, near_block = finish(arrived, True, j, partial)
+            blocks = finish(arrived, rounds, j, partial)
+            partial, (late_block, near_block, *other) = blocks[:3], blocks[3:]
+            rest += other
             sent = lax.ppermute(late_block, "path", cross)
             moved.append((sent, lax.ppermute(sent, "path", swap)))
             beside.append(lax.ppermute(near_block, "path", swap))
+        extra = [(None, None)] * owned_sets
+        if others:
+            if others < owned_sets:
+                chosen = rest[-1]
+                for j in range(owned_sets - 1):
+                    chosen = jnp.where(needed[j], rest[j], chosen)
+                rest = [chosen]
+            sent = [lax.ppermute(block, "path", cross) for block in rest]
+            sent = [(block, lax.ppermute(block, "path", swap)) for block in sent]
+            extra = sent if others == owned_sets else sent * owned_sets
         experts, inertias, returned = partial
         for j in range(owned_sets):
             returned = place_block(scalars, returned, beside[j], j, owned_sets, 1)
         for j in range(owned_sets):
             for turn in range(2):
                 returned = place_far(
-                    scalars, returned, moved[j][turn], still[turn], mine, j, owned_sets, turn
+                    scalars,
+                    returned,
+                    moved[j][turn],
+                    still[turn],
+                    mine,
+                    extra[j][turn],
+                    j,
+                    owned_sets,
+                    turn,
                 )
         return experts, inertias, returned
 
+    def survivors(rounds):
+        base = pick_early(scalars, common, inertia)
+        early = lax.ppermute(base, "path", cross)
+        arrived, mine = run_survivors(plan, rounds, flags, x, g, r, m, v)
+        if rounds == 1:
+            return exchange(rounds, 0, arrived, mine, early, None)
+        needed = []
+        for chip in range(2):
+            part = slice(chip * 2 * owned_sets, (chip + 1) * 2 * owned_sets)
+            differ = trajectory_membership[0::2, part] != trajectory_membership[1::2, part]
+            full = flags[2 * chip] + flags[2 * chip + 1] == 2
+            needed.append(full & differ[0] & differ[1])
+        needed = jnp.concatenate(needed).reshape(path_count, owned_sets)
+        most = jnp.max(jnp.sum(needed.astype(jnp.int32), axis=1))
+        own = needed[lax.axis_index("path")]
+        return lax.switch(
+            jnp.minimum(most, 2),
+            [
+                functools.partial(exchange, rounds, count)
+                for count in (0, min(1, owned_sets), owned_sets)
+            ],
+            arrived,
+            mine,
+            early,
+            own,
+        )
+
     if path_count == 4 and choices == 2:
-        lone = jnp.max(flags.reshape(2, 2).sum(axis=1)) <= 1
-        return lax.cond(lone, single, both)
+        lone = (flags[0] + flags[1] <= 1) & (flags[2] + flags[3] <= 1)
+        return lax.cond(lone, lambda: survivors(1), lambda: survivors(2))
     return both()
 
 

time: 228 us -> 220 us (0.965)
  Pallas kernels: 178 us -> 168 us
    pallas_call x1, Pallas kernels: 134 us -> 126 us  [run_survivors(): pl.pallas_call(functools.partial(survivor_kernel, plan, rounds), out_shap...]
    pallas_call x9, Pallas kernels: 44.4 us -> 42.1 us  [local_call(): pl.pallas_call(body, grid_spec=pltpu.PrefetchScalarGridSpec(num_scalar_pr...]
  transfers between devices with their start and end apart: 8 -> 8, of which waited for: 2 -> 2; matrix products, arithmetic and copies ran while one was open for 0% -> 0% of each run, Pallas kernels for 74% -> 72%
where the time goes in v1:
time: 220 us
  Pallas kernels  168 us (76%)
  waiting for transfers between devices  36.6 us (17%)
  local copies, waits for them, and re-layouts  5.82 us (3%)
  starting transfers between devices  5.54 us (3%)
  between operations  3.27 us (1%)
    pallas_call x1, Pallas kernels, run_survivors(): pl.pallas_call(functools.partial(survivor_kernel, plan, rounds), out_shap...  126 us
    pallas_call x9, Pallas kernels, local_call(): pl.pallas_call(body, grid_spec=pltpu.PrefetchScalarGridSpec(num_scalar_pr...  42.1 us
    ppermute x2, waiting for transfers between devices, exchange(): sent = lax.ppermute(late_block, 'path', cross)  36.6 us
    cond x16, local copies, waits for them, and re-layouts  4.43 us
  transfers between devices with their start and end apart: 8, of which 2 were waited for; matrix products, arithmetic and copies ran while one was open for 0% of the time, Pallas kernels for 72%

profile of v1, /device:TPU:0, one launch (start us, length us, event | category | flops | bytes accessed | tf_op | source)
XLA Modules:
  0.0 219.9 jit_solution(11980532530423001861)
XLA Ops:
  0.6 1.4 fusion.1
  4.7 215.2 %conditional.2 = ((f32[2,2,128,4096]{3,2,1,0:T(8,128)}, f32[2,2,128,4096]{3,2,1,0:T(8,128)}, bf16[1,8,128,4096]{3,2,1,0:T(8,128)(2,1)})) conditional(s32[]{:T(128)} %bitcast.3, (s32[4]{0:T(128)}, s32[4,8]{1,0:T(4,128)}, s32[1]{0:T(128)}, f32[2,2,128,4096]{3,2,1,0:T(8,128)}, f32[2,2,128,4096]{3,2,1,0:T(8,128)}, /*index=5*/bf16[192,2048]{1,0:T(8,128)(2,1)}, ...), branch_computations={%region_0.6_spmd, %region_6.7_spmd} | conditional | flops 51735166976 | bytes 316672064 | solution.py:1153
  4.9 6.2 %branch_1_fun.27 = bf16[2,128,4096]{2,1,0:T(8,128)(2,1)} custom-call(s32[4,8]{1,0:T(4,128)} %get-tuple-element.174.member_ref, s32[4]{0:T(128)} %get-tuple-element.175.flags_ref, s32[1]{0:T(128)} %get-tuple-element.176.spot_ref, f32[2,2,128,4096]{3,2,1,0:T(8,128)} %get-tuple-element.183.common_ref, f32[2,2,128,4096]{3,2,1,0:T(8,128)} %get-tuple-element.184.inertia_ref), custom_call_target="tpu_custom_call" | custom-call | flops 16777216 | bytes 16777216 | tf_op jit(solution)/shard_map/cond/branch_1_fun/pallas_call | solution.py:839
  11.2 3.0 %collective-permute-start.20 = (bf16[2,128,4096]{2,1,0:T(8,128)(2,1)}, bf16[2,128,4096]{2,1,0:T(8,128)(2,1)}, u32[]{:S(2)}, u32[]{:S(2)}) collective-permute-start(bf16[2,128,4096]{2,1,0:T(8,128)(2,1)} %branch_1_fun.27), channel_id=1, source_target_pairs={{0,16},{8,24},{16,0},{24,8},{1,17},{9,25},{17,1},{25,9},{2,18},{10... | collective-permute-start | bytes 6291464 | tf_op jit(solution)/shard_map/cond/branch_1_fun/ppermute | solution.py:1126
  14.2 126.2 %survivors.3 = (bf16[2,256,4096]{2,1,0:T(8,128)(2,1)}, bf16[512,4096]{1,0:T(8,128)(2,1)}) custom-call(s32[4]{0:T(128)} %get-tuple-element.175.flags_ref, bf16[192,2048]{1,0:T(8,128)(2,1)} %get-tuple-element.177.x_hbm, bf16[192,2048]{1,0:T(8,128)(2,1)} %get-tuple-element.178.g_hbm, bf16[1024,4096]{1,0:T(8,128)(2,1)} %get-tuple-element.179.r_hbm, ...), custom_call_target="tpu_custom_call" | custom-call | flops 25769803776 | bytes 33554432 | tf_op jit(solution)/shard_map/cond/branch_1_fun/survivors/pallas_call | solution.py:798
  140.4 0.0 copy-start.9
  140.4 8.6 %branch_1_fun.25 = (f32[2,2,128,4096]{3,2,1,0:T(8,128)}, f32[2,2,128,4096]{3,2,1,0:T(8,128)}, bf16[1,8,128,4096]{3,2,1,0:T(8,128)(2,1)}, bf16[128,4096]{1,0:T(8,128)(2,1)}, bf16[128,4096]{1,0:T(8,128)(2,1)}) custom-call(s32[4,8]{1,0:T(4,128)} %get-tuple-element.174.member_ref, s32[4]{0:T(128)} %get-tuple-element.175.flags_ref, ...), custom_call_target="tpu_custom_call" | custom-call | flops 20971520 | bytes 20971520 | tf_op jit(solution)/shard_map/cond/branch_1_fun/pallas_call | solution.py:839
  149.1 1.7 collective-permute-start.22
  150.7 8.4 %branch_1_fun.26 = (f32[2,2,128,4096]{3,2,1,0:T(8,128)}, f32[2,2,128,4096]{3,2,1,0:T(8,128)}, bf16[1,8,128,4096]{3,2,1,0:T(8,128)(2,1)}, bf16[128,4096]{1,0:T(8,128)(2,1)}, bf16[128,4096]{1,0:T(8,128)(2,1)}) custom-call(s32[4,8]{1,0:T(4,128)S(1)} %copy-done.9, s32[4]{0:T(128)S(1)} %copy-done.32, ...), custom_call_target="tpu_custom_call", output_to_operand_aliasing={{0}: (6, {}), {1}: (7, {}), {2}: (8, {})} | custom-call | flops 46137344 | bytes 46137344 | tf_op jit(solution)/shard_map/cond/branch_1_fun/pallas_call | solution.py:839
  159.1 0.4 collective-permute-start.18
  159.5 0.2 collective-permute-start.25
  159.7 0.3 collective-permute-start.24
  160.0 15.3 %collective-permute-done.22.late_ref = bf16[128,4096]{1,0:T(8,128)(2,1)S(1)} collective-permute-done((bf16[128,4096]{1,0:T(8,128)(2,1)}, bf16[128,4096]{1,0:T(8,128)(2,1)S(1)}, u32[]{:S(2)}, u32[]{:S(2)}) %collective-permute-start.22) | collective-permute-done | bytes 1048608 | tf_op jit(solution)/shard_map/cond/branch_1_fun/ppermute | solution.py:1093
  175.3 21.3 %collective-permute-done.18.late_ref = bf16[128,4096]{1,0:T(8,128)(2,1)S(1)} collective-permute-done((bf16[128,4096]{1,0:T(8,128)(2,1)}, bf16[128,4096]{1,0:T(8,128)(2,1)S(1)}, u32[]{:S(2)}, u32[]{:S(2)}) %collective-permute-start.18) | collective-permute-done | bytes 1048608 | tf_op jit(solution)/shard_map/cond/branch_1_fun/ppermute | solution.py:1093
  196.6 2.6 %branch_1_fun.28._ = bf16[1,8,128,4096]{3,2,1,0:T(8,128)(2,1)} custom-call(s32[4,8]{1,0:T(4,128)S(1)} %copy-done.9, s32[4]{0:T(128)S(1)} %copy-done.32, s32[1]{0:T(128)} %get-tuple-element.176.spot_ref, bf16[128,4096]{1,0:T(8,128)(2,1)} %collective-permute-done.25.block_ref, ...), custom_call_target="tpu_custom_call", output_to_operand_aliasing={{}: (4, {})} | custom-call | flops 9437184 | bytes 9437184 | tf_op jit(solution)/shard_map/cond/branch_1_fun/pallas_call | solution.py:839
  199.3 1.0 copy-done.27
  200.2 2.6 %branch_1_fun.29.refs_0_ = bf16[1,8,128,4096]{3,2,1,0:T(8,128)(2,1)} custom-call(s32[4,8]{1,0:T(4,128)S(1)} %copy-done.9, s32[4]{0:T(128)S(1)} %copy-done.32, s32[1]{0:T(128)} %get-tuple-element.176.spot_ref, bf16[128,4096]{1,0:T(8,128)(2,1)} %copy-done.27, bf16[1,8,128,4096]{3,2,1,0:T(8,128)(2,1)} %branch_1_fun.28._), custom_call_target="tpu_custom_call", output_to_operand_aliasing={{}: (4, {})} | custom-call | flops 9437184 | bytes 9437184 | tf_op jit(solution)/shard_map/cond/branch_1_fun/pallas_call | solution.py:839
  202.9 3.4 %branch_1_fun.30.refs_0_ = bf16[1,8,128,4096]{3,2,1,0:T(8,128)(2,1)} custom-call(s32[4,8]{1,0:T(4,128)S(1)} %copy-done.9, s32[4]{0:T(128)S(1)} %copy-done.32, s32[1]{0:T(128)} %get-tuple-element.176.spot_ref, bf16[128,4096]{1,0:T(8,128)(2,1)} %copy-done.16, bf16[2,128,4096]{2,1,0:T(8,128)(2,1)} %collective-permute-done.20.early_ref, ...), custom_call_target="tpu_custom_call", output_to_operand_aliasing={{}: (6, {})} | custom-call | flops 15728640 | bytes 15728640 | tf_op jit(solution)/shard_map/cond/branch_1_fun/pallas_call | solution.py:839
  206.3 1.1 copy-done.24
  207.3 1.4 copy-done.1
  208.7 3.4 %branch_1_fun.31.refs_0_ = bf16[1,8,128,4096]{3,2,1,0:T(8,128)(2,1)} custom-call(s32[4,8]{1,0:T(4,128)S(1)} %copy-done.9, s32[4]{0:T(128)S(1)} %copy-done.32, s32[1]{0:T(128)} %get-tuple-element.176.spot_ref, bf16[128,4096]{1,0:T(8,128)(2,1)} %copy-done.24, bf16[2,128,4096]{2,1,0:T(8,128)(2,1)} %copy-done.1, ...), custom_call_target="tpu_custom_call", output_to_operand_aliasing={{}: (6, {})} | custom-call | flops 15728640 | bytes 15728640 | tf_op jit(solution)/shard_map/cond/branch_1_fun/pallas_call | solution.py:839
  212.1 3.4 %branch_1_fun.32.refs_0_ = bf16[1,8,128,4096]{3,2,1,0:T(8,128)(2,1)} custom-call(s32[4,8]{1,0:T(4,128)S(1)} %copy-done.9, s32[4]{0:T(128)S(1)} %copy-done.32, s32[1]{0:T(128)} %get-tuple-element.176.spot_ref, bf16[128,4096]{1,0:T(8,128)(2,1)} %copy-done.20, bf16[2,128,4096]{2,1,0:T(8,128)(2,1)} %collective-permute-done.20.early_ref, ...), custom_call_target="tpu_custom_call", output_to_operand_aliasing={{}: (6, {})} | custom-call | flops 15728640 | bytes 15728640 | tf_op jit(solution)/shard_map/cond/branch_1_fun/pallas_call | solution.py:839
  215.5 1.0 copy-done.22
  216.5 3.4 %branch_1_fun.33 = bf16[1,8,128,4096]{3,2,1,0:T(8,128)(2,1)} custom-call(s32[4,8]{1,0:T(4,128)S(1)} %copy-done.9, s32[4]{0:T(128)S(1)} %copy-done.32, s32[1]{0:T(128)} %get-tuple-element.176.spot_ref, bf16[128,4096]{1,0:T(8,128)(2,1)} %copy-done.22, bf16[2,128,4096]{2,1,0:T(8,128)(2,1)} %copy-done.1, ...), custom_call_target="tpu_custom_call", output_to_operand_aliasing={{}: (6, {})} | custom-call | flops 15728640 | bytes 15728640 | tf_op jit(solution)/shard_map/cond/branch_1_fun/pallas_call | solution.py:839
  (20 shorter events, 0.0 us)
Async XLA Ops:
  11.2 139.6 %collective-permute-start.20 = (bf16[2,128,4096]{2,1,0:T(8,128)(2,1)}, bf16[2,128,4096]{2,1,0:T(8,128)(2,1)}, u32[]{:S(2)}, u32[]{:S(2)}) collective-permute-start(bf16[2,128,4096]{2,1,0:T(8,128)(2,1)} %branch_1_fun.27), channel_id=1, source_target_pairs={{0,16},{8,24},{16,0},{24,8},{1,17},{9,25},{17,1},{25,9},{2,18},{10... | collective-permute-start | bytes 6291464 | tf_op jit(solution)/shard_map/cond/branch_1_fun/ppermute | solution.py:1126
  140.4 10.3 %copy-start.9 = (s32[4,8]{1,0:T(4,128)S(1)}, s32[4,8]{1,0:T(4,128)}, u32[]{:S(2)}) copy-start(s32[4,8]{1,0:T(4,128)} %get-tuple-element.174.member_ref) | copy-start | bytes 388 | tf_op jit(solution)/shard_map/cond
  140.4 10.3 %copy-start.32 = (s32[4]{0:T(128)S(1)}, s32[4]{0:T(128)}, u32[]{:S(2)}) copy-start(s32[4]{0:T(128)} %get-tuple-element.175.flags_ref) | copy-start | bytes 52 | tf_op jit(solution)/shard_map/cond
  149.1 26.2 %collective-permute-start.22 = (bf16[128,4096]{1,0:T(8,128)(2,1)}, bf16[128,4096]{1,0:T(8,128)(2,1)S(1)}, u32[]{:S(2)}, u32[]{:S(2)}) collective-permute-start(bf16[128,4096]{1,0:T(8,128)(2,1)} %get-tuple-element.192), channel_id=1, source_target_pairs={{0,16},{8,24},{16,0},{24,8},{1,17},{9,25},{17,1},{25,9},{2,18},{10... | collective-permute-start | bytes 3145736 | tf_op jit(solution)/shard_map/cond/branch_1_fun/ppermute | solution.py:1093
  150.7 55.6 %collective-permute-start.21 = (bf16[2,128,4096]{2,1,0:T(8,128)(2,1)}, bf16[2,128,4096]{2,1,0:T(8,128)(2,1)S(1)}, u32[]{:S(2)}, u32[]{:S(2)}) collective-permute-start(bf16[2,128,4096]{2,1,0:T(8,128)(2,1)} %collective-permute-done.20.early_ref), channel_id=1, source_target_pairs={{0,8},{8,0},{16,24},{24,16},{1,9},{9,1},{17,25},{25,17},{2,10},{10... | collective-permute-start | bytes 6291464 | tf_op jit(solution)/shard_map/cond/branch_1_fun/ppermute | solution.py:1087
  159.1 37.5 %collective-permute-start.18 = (bf16[128,4096]{1,0:T(8,128)(2,1)}, bf16[128,4096]{1,0:T(8,128)(2,1)S(1)}, u32[]{:S(2)}, u32[]{:S(2)}) collective-permute-start(bf16[128,4096]{1,0:T(8,128)(2,1)} %get-tuple-element.190), channel_id=1, source_target_pairs={{0,16},{8,24},{16,0},{24,8},{1,17},{9,25},{17,1},{25,9},{2,18},{10... | collective-permute-start | bytes 3145736 | tf_op jit(solution)/shard_map/cond/branch_1_fun/ppermute | solution.py:1093
  159.5 37.1 %collective-permute-start.25 = (bf16[128,4096]{1,0:T(8,128)(2,1)}, bf16[128,4096]{1,0:T(8,128)(2,1)}, u32[]{:S(2)}, u32[]{:S(2)}) collective-permute-start(bf16[128,4096]{1,0:T(8,128)(2,1)} %get-tuple-element.194), channel_id=1, source_target_pairs={{0,8},{8,0},{16,24},{24,16},{1,9},{9,1},{17,25},{25,17},{2,10},{10... | collective-permute-start | bytes 3145736 | tf_op jit(solution)/shard_map/cond/branch_1_fun/ppermute | solution.py:1095
  159.7 39.5 %collective-permute-start.24 = (bf16[128,4096]{1,0:T(8,128)(2,1)}, bf16[128,4096]{1,0:T(8,128)(2,1)S(1)}, u32[]{:S(2)}, u32[]{:S(2)}) collective-permute-start(bf16[128,4096]{1,0:T(8,128)(2,1)} %get-tuple-element.193), channel_id=1, source_target_pairs={{0,8},{8,0},{16,24},{24,16},{1,9},{9,1},{17,25},{25,17},{2,10},{10... | collective-permute-start | bytes 3145736 | tf_op jit(solution)/shard_map/cond/branch_1_fun/ppermute | solution.py:1095
  175.3 24.0 %copy-start.16 = (bf16[128,4096]{1,0:T(8,128)(2,1)}, bf16[128,4096]{1,0:T(8,128)(2,1)S(1)}, u32[]{:S(2)}) copy-start(bf16[128,4096]{1,0:T(8,128)(2,1)S(1)} %collective-permute-done.22.late_ref) | copy-start | bytes 3145732 | tf_op jit(solution)/shard_map/cond
  175.3 31.0 %collective-permute-start.23 = (bf16[128,4096]{1,0:T(8,128)(2,1)S(1)}, bf16[128,4096]{1,0:T(8,128)(2,1)S(1)}, u32[]{:S(2)}, u32[]{:S(2)}) collective-permute-start(bf16[128,4096]{1,0:T(8,128)(2,1)S(1)} %collective-permute-done.22.late_ref), channel_id=1, source_target_pairs={{0,8},{8,0},{16,24},{24,16},{1,9},{9,1},{17,25},{25,17},{2,10},{10... | collective-permute-start | bytes 3145736 | tf_op jit(solution)/shard_map/cond/branch_1_fun/ppermute | solution.py:1094
  196.6 2.6 %copy-start.20 = (bf16[128,4096]{1,0:T(8,128)(2,1)}, bf16[128,4096]{1,0:T(8,128)(2,1)S(1)}, u32[]{:S(2)}) copy-start(bf16[128,4096]{1,0:T(8,128)(2,1)S(1)} %collective-permute-done.18.late_ref) | copy-start | bytes 3145732 | tf_op jit(solution)/shard_map/cond
  196.6 18.9 %collective-permute-start.19 = (bf16[128,4096]{1,0:T(8,128)(2,1)S(1)}, bf16[128,4096]{1,0:T(8,128)(2,1)S(1)}, u32[]{:S(2)}, u32[]{:S(2)}) collective-permute-start(bf16[128,4096]{1,0:T(8,128)(2,1)S(1)} %collective-permute-done.18.late_ref), channel_id=1, source_target_pairs={{0,8},{8,0},{16,24},{24,16},{1,9},{9,1},{17,25},{25,17},{2,10},{10... | collective-permute-start | bytes 3145736 | tf_op jit(solution)/shard_map/cond/branch_1_fun/ppermute | solution.py:1094
  199.3 1.0 copy-start.27
  206.3 1.1 copy-start.24
  207.3 1.4 copy-start.1
  215.5 1.0 copy-start.22

commit v2 on v1

--- a/solution.py
+++ b/solution.py
@@ -450,13 +450,28 @@
 
 
 def survivor_kernel(
-    plan, rounds, flags_ref, x_hbm, g_hbm, r_hbm, m_hbm, v_hbm, arr_hbm, own_hbm, *scratch
+    plan,
+    rounds,
+    member_ref,
+    flags_ref,
+    x_hbm,
+    g_hbm,
+    r_hbm,
+    m_hbm,
+    v_hbm,
+    common_hbm,
+    inertia_hbm,
+    arr_hbm,
+    own_hbm,
+    early_hbm,
+    *scratch,
 ):
     (xg, params, hidden, first, second, pseudo, raw, swapped) = scratch[:8]
-    (cross_in, own_in, cross_out, own_out) = scratch[8:12]
+    (cross_in, own_in, cross_out, own_out, shown) = scratch[8:13]
     (load_sem, moment_sem, send_sem, recv_sem, side_send, side_recv, out_send, out_recv, keep_sem) = (
-        scratch[12:]
-    )
+        scratch[13:22]
+    )
+    (shown_sem, early_sem) = scratch[22:]
     n, shard, half = plan.ring, plan.shard, plan.half
     features, owned, tile, tiles = plan.features, plan.owned, plan.tile, plan.tiles
     pieces, slots = plan.pieces, plan.slots
@@ -546,6 +561,59 @@
             device_id_type=MESH,
         )
 
+    def show(e):
+        return (
+            pltpu.make_async_copy(
+                common_hbm.at[:, :, :, cols_of(e)], shown.at[0], shown_sem.at[0]
+            ),
+            pltpu.make_async_copy(
+                inertia_hbm.at[:, :, :, cols_of(e)], shown.at[1], shown_sem.at[1]
+            ),
+        )
+
+    def early_copy(e):
+        return pltpu.make_async_remote_copy(
+            src_ref=cross_out.at[e],
+            dst_ref=early_hbm.at[0, :, cols_of(e)],
+            send_sem=early_sem.at[0, e],
+            recv_sem=early_sem.at[1, e],
+            device_id={"path": far + core, "fsdp": place},
+            device_id_type=MESH,
+        )
+
+    def early_share(e):
+        return pltpu.make_async_remote_copy(
+            src_ref=early_hbm.at[0, :, cols_of(e)],
+            dst_ref=early_hbm.at[1, :, cols_of(e)],
+            send_sem=early_sem.at[2, e],
+            recv_sem=early_sem.at[3, e],
+            device_id={"path": sibling, "fsdp": place},
+            device_id_type=MESH,
+        )
+
+    sets, units = shown.shape[1], shown.shape[3]
+
+    def early_tile(e, carry):
+        for load in show(e):
+            load.wait()
+        for j in range(sets):
+            late = late_of(member_ref, flags_ref, path * sets + j, chip)
+            common = jnp.where(late == 0, shown[0, j, 1], shown[0, j, 0])
+            inertia = jnp.where(late == 0, shown[1, j, 1], shown[1, j, 0])
+            base, _ = refreshed(0.0, 1.0, common, inertia)
+            cross_out[e, j * units : (j + 1) * units] = base.astype(jnp.bfloat16)
+        early_copy(e).start()
+
+        @pl.when(e + 1 < tiles)
+        def _():
+            for load in show(e + 1):
+                load.start()
+
+        return carry
+
+    for load in show(0):
+        load.start()
+
     def begin(turn):
         for copy in ring_copies(turn, 1):
             copy.start()
@@ -621,6 +689,11 @@
             cross_copy(index - tiles).wait_send()
             near_copy(index - tiles).wait()
 
+        @pl.when(index < tiles)
+        def _():
+            early_copy(index).wait()
+            early_share(index).start()
+
         slot, t = index % slots, index % tiles
         share_copy(index, 0).wait_recv()
         cross_out[t] = jnp.where(mine, pseudo[slot, rows_of(far + core)], cross_in[index])
@@ -681,6 +754,7 @@
         return carry
 
     spread = -(-tiles // 4)
+    each = -(-tiles // n)
     last = rounds * n
 
     def stage(i, carry):
@@ -725,6 +799,9 @@
             )
             begun = jnp.where((turn == 1) & (k < 6), jnp.where(k == 5, 2, 0), begun)
             ended = jnp.where((turn == 1) & (k < 5), jnp.where(k == 4, 2, 0), ended)
+        lax.fori_loop(
+            jnp.minimum(i * each, tiles), jnp.minimum((i + 1) * each, tiles), early_tile, 0
+        )
         lax.fori_loop(low, high, grad_tile, 0)
 
         def ready(j, inner):
@@ -760,13 +837,17 @@
             near_copy(index).wait()
             cross_copy(index).wait_send()
 
+        @pl.when(index < tiles)
+        def _():
+            early_share(index).wait()
+
         cross_copy(index).wait_recv()
         return carry
 
     lax.fori_loop(0, rounds * tiles, drain, 0)
 
 
-def run_survivors(plan, rounds, flags, x, g, r, m, v):
+def run_survivors(plan, rounds, member, flags, x, g, r, m, v, common, inertia):
     bf16, dma = jnp.bfloat16, pltpu.SemaphoreType.DMA
     width, tile, tiles = plan.width, plan.tile, plan.tiles
     served = pltpu.VMEM((rounds * tiles, plan.owned, tile), bf16)
@@ -784,6 +865,7 @@
         served,
         sent,
         sent,
+        pltpu.VMEM((2,) + common.shape[:3] + (tile,), jnp.float32),
         dma((5,)),
         dma((2, 2)),
         dma((rounds, 2 * plan.pieces, plan.ring)),
@@ -793,6 +875,8 @@
         dma((rounds * tiles, 3)),
         dma((rounds * tiles, 3)),
         dma((2, rounds * tiles)),
+        dma((2,)),
+        dma((4, tiles)),
     ]
     anywhere = pl.BlockSpec(memory_space=pl.ANY)
     return pl.pallas_call(
@@ -800,9 +884,10 @@
         out_shape=[
             jax.ShapeDtypeStruct((2 * rounds, plan.owned, width), bf16),
             jax.ShapeDtypeStruct((2 * rounds * plan.owned, width), bf16),
+            jax.ShapeDtypeStruct((2, plan.owned, width), bf16),
         ],
-        in_specs=[pl.BlockSpec(memory_space=pltpu.SMEM)] + [anywhere] * 5,
-        out_specs=[anywhere] * 2,
+        in_specs=[pl.BlockSpec(memory_space=pltpu.SMEM)] * 2 + [anywhere] * 7,
+        out_specs=[anywhere] * 3,
         scratch_shapes=scratch,
         compiler_params=pltpu.CompilerParams(
             collective_id=rounds, has_side_effects=True, vmem_limit_bytes=67043328
@@ -813,7 +898,7 @@
             transcendentals=0,
         ),
         name="survivors",
-    )(flags, x, g, r, m, v)
+    )(member, flags, x, g, r, m, v, common, inertia)
 
 
 def refreshed(total, tally, common, inertia):
@@ -843,36 +928,12 @@
         ),
         out_shape=out_shape,
         input_output_aliases=aliases or {},
-        compiler_params=pltpu.CompilerParams(vmem_limit_bytes=56 * 1024 * 1024),
+        compiler_params=pltpu.CompilerParams(vmem_limit_bytes=67043328),
         cost_estimate=pl.CostEstimate(flops=size, bytes_accessed=size, transcendentals=0),
     )(*scalars, *arrays)
 
 
 ANYWHERE = pl.BlockSpec(memory_space=pl.ANY)
-
-
-def pick_early(scalars, common, inertia):
-    sets, _, units, width = common.shape
-    step = divisor(width, 2048)
-
-    def body(member_ref, flags_ref, spot_ref, common_ref, inertia_ref, out):
-        expert, _ = refreshed(0.0, 1.0, common_ref[0, 0], inertia_ref[0, 0])
-        out[0] = expert.astype(jnp.bfloat16)
-
-    def at(j, t, member_ref, flags_ref, spot_ref):
-        spot = spot_ref[0]
-        late = late_of(member_ref, flags_ref, spot * sets + j, spot // 2)
-        return (j, 1 - late, 0, t)
-
-    return local_call(
-        body,
-        (sets, width // step),
-        [pl.BlockSpec((1, 1, units, step), at)] * 2,
-        pl.BlockSpec((1, units, step), lambda j, t, *_: (j, 0, t)),
-        jax.ShapeDtypeStruct((sets, units, width), jnp.bfloat16),
-        scalars,
-        [common, inertia],
-    )
 
 
 def finish_set(scalars, common, inertia, arrived, j, rounds, paths, shape, partial):
@@ -968,7 +1029,7 @@
     return changed & (member[far, at] != member[far + 1, at])
 
 
-def place_far(scalars, returned, late_block, early_block, mine, other_block, j, sets, turn):
+def place_far(scalars, returned, late_block, early_block, mine, j, sets, turn):
     _, _, units, width = returned.shape
     step = divisor(width, 2048)
 
@@ -986,9 +1047,6 @@
         late = late_of(member_ref, flags_ref, at, 1 - spot // 2)
         quiet = early_ref[0].astype(jnp.float32) - gain * mine_ref[...].astype(jnp.float32)
         quiet = quiet.astype(jnp.bfloat16)
-        if other_block is not None:
-            sent = needs_other(member_ref, flags_ref, at, 1 - spot // 2)
-            quiet = jnp.where(sent, refs[0][...], quiet)
         out[0, 0] = jnp.where(member_ref[spot, at] == late, late_ref[...], quiet)
 
     def mine_at(t, m, flags_ref, spot_ref):
@@ -1001,12 +1059,9 @@
     arrays = [late_block, early_block, mine]
     specs = [
         flat,
-        pl.BlockSpec((1, units, step), lambda t, *_: (j, 0, t)),
+        pl.BlockSpec((1, units, step), lambda t, *_: (turn, j, t)),
         pl.BlockSpec((units, step), mine_at),
     ]
-    if other_block is not None:
-        arrays.append(other_block)
-        specs.append(flat)
     return local_call(
         body,
         (width // step,),
@@ -1016,6 +1071,43 @@
         scalars,
         arrays + [returned],
         {3 + len(arrays): 0},
+    )
+
+
+def place_other(scalars, returned, block, j, sets, turn):
+    _, _, units, width = returned.shape
+    step = divisor(width, 2048)
+
+    def place(member_ref, flags_ref, spot):
+        first = (2 * (1 - spot // 2) + ((spot % 2) ^ turn)) * sets
+        if j is not None:
+            return first + j
+        at = first + sets - 1
+        for i in range(sets - 1):
+            needed = needs_other(member_ref, flags_ref, first + i, 1 - spot // 2)
+            at = jnp.where(needed, first + i, at)
+        return at
+
+    def body(member_ref, flags_ref, spot_ref, block_ref, before, out):
+        spot = spot_ref[0]
+        at = place(member_ref, flags_ref, spot)
+        late = late_of(member_ref, flags_ref, at, 1 - spot // 2)
+        sent = needs_other(member_ref, flags_ref, at, 1 - spot // 2)
+        wanted = sent & (member_ref[spot, at] != late)
+        out[0, 0] = jnp.where(wanted, block_ref[...], before[0, 0])
+
+    spec = pl.BlockSpec(
+        (1, 1, units, step), lambda t, m, f, spot_ref: (0, place(m, f, spot_ref[0]), 0, t)
+    )
+    return local_call(
+        body,
+        (width // step,),
+        [pl.BlockSpec((units, step), lambda t, *_: (0, t)), spec],
+        spec,
+        jax.ShapeDtypeStruct(returned.shape, jnp.bfloat16),
+        scalars,
+        [block, returned],
+        {4: 0},
     )
 
 
@@ -1084,7 +1176,6 @@
     swap = [(p, p ^ 1) for p in range(path_count)]
 
     def exchange(rounds, others, arrived, mine, early, needed):
-        still = (early, lax.ppermute(early, "path", swap))
         moved, beside, rest, partial = [], [], [], ()
         for j in range(owned_sets):
             blocks = finish(arrived, rounds, j, partial)
@@ -1093,7 +1184,7 @@
             sent = lax.ppermute(late_block, "path", cross)
             moved.append((sent, lax.ppermute(sent, "path", swap)))
             beside.append(lax.ppermute(near_block, "path", swap))
-        extra = [(None, None)] * owned_sets
+        extra = []
         if others:
             if others < owned_sets:
                 chosen = rest[-1]
@@ -1101,8 +1192,7 @@
                     chosen = jnp.where(needed[j], rest[j], chosen)
                 rest = [chosen]
             sent = [lax.ppermute(block, "path", cross) for block in rest]
-            sent = [(block, lax.ppermute(block, "path", swap)) for block in sent]
-            extra = sent if others == owned_sets else sent * owned_sets
+            extra = [(block, lax.ppermute(block, "path", swap)) for block in sent]
         experts, inertias, returned = partial
         for j in range(owned_sets):
             returned = place_block(scalars, returned, beside[j], j, owned_sets, 1)
@@ -1112,29 +1202,31 @@
                     scalars,
                     returned,
                     moved[j][turn],
-                    still[turn],
+                    early,
                     mine,
-                    extra[j][turn],
                     j,
                     owned_sets,
                     turn,
                 )
+        for j, pair in enumerate(extra):
+            at = j if others == owned_sets else None
+            for turn in range(2):
+                returned = place_other(scalars, returned, pair[turn], at, owned_sets, turn)
         return experts, inertias, returned
 
     def survivors(rounds):
-        base = pick_early(scalars, common, inertia)
-        early = lax.ppermute(base, "path", cross)
-        arrived, mine = run_survivors(plan, rounds, flags, x, g, r, m, v)
+        arrived, mine, early = run_survivors(
+            plan, rounds, trajectory_membership, flags, x, g, r, m, v, common, inertia
+        )
         if rounds == 1:
             return exchange(rounds, 0, arrived, mine, early, None)
-        needed = []
-        for chip in range(2):
-            part = slice(chip * 2 * owned_sets, (chip + 1) * 2 * owned_sets)
-            differ = trajectory_membership[0::2, part] != trajectory_membership[1::2, part]
-            full = flags[2 * chip] + flags[2 * chip + 1] == 2
-            needed.append(full & differ[0] & differ[1])
-        needed = jnp.concatenate(needed).reshape(path_count, owned_sets)
-        most = jnp.max(jnp.sum(needed.astype(jnp.int32), axis=1))
+        pairs = trajectory_membership.reshape(2, 2, set_count)
+        differ = (pairs[0, 0] != pairs[0, 1]) & (pairs[1, 0] != pairs[1, 1])
+        alive = jnp.where(
+            jnp.arange(set_count) < 2 * owned_sets, flags[0] + flags[1], flags[2] + flags[3]
+        )
+        needed = (differ & (alive == 2)).reshape(path_count, owned_sets)
+        most = jnp.max(sum(needed[:, j].astype(jnp.int32) for j in range(owned_sets)))
         own = needed[lax.axis_index("path")]
         return lax.switch(
             jnp.minimum(most, 2),

time: 220 us -> 210 us (0.955)
  local copies, waits for them, and re-layouts: 5.82 us -> 1.4 us
  starting transfers between devices: 5.54 us -> 2.54 us
    pallas_call x9 -> x8, Pallas kernels: 42.1 us -> 36.6 us  [local_call(): pl.pallas_call(body, grid_spec=pltpu.PrefetchScalarGridSpec(num_scalar_pr...]
    cond x16 -> x0, local copies, waits for them, and re-layouts: 4.43 us -> none
    ppermute x2 -> x0, starting transfers between devices: 3 us -> none  [the longest x1 3 us: survivors(): early = lax.ppermute(base, 'path', cross)]
    pallas_call x1, Pallas kernels: 126 us -> 129 us  [run_survivors(): pl.pallas_call(functools.partial(survivor_kernel, plan, rounds), out_shap...]
  transfers between devices with their start and end apart: 8 -> 6, of which waited for: 2 -> 2; matrix products, arithmetic and copies ran while one was open for 0% -> 0% of each run, Pallas kernels for 72% -> 12%
where the time goes in v2:
time: 210 us; the launch traced here: 209 us
  Pallas kernels  166 us (79%)
  waiting for transfers between devices  36.1 us (17%)
  between operations  3.21 us (2%)
  starting transfers between devices  2.54 us (1%)
    pallas_call x1, Pallas kernels, run_survivors(): pl.pallas_call(functools.partial(survivor_kernel, plan, rounds), out_shap...  129 us
    pallas_call x8, Pallas kernels, local_call(): pl.pallas_call(body, grid_spec=pltpu.PrefetchScalarGridSpec(num_scalar_pr...  36.6 us
    ppermute x2, waiting for transfers between devices, exchange(): sent = lax.ppermute(late_block, 'path', cross)  36.1 us
  transfers between devices with their start and end apart: 6, of which 2 were waited for; matrix products, arithmetic and copies ran while one was open for 0% of the time, Pallas kernels for 12%

profile of v2, /device:TPU:0, one launch (start us, length us, event | category | flops | bytes accessed | tf_op | source)
XLA Modules:
  0.0 209.1 jit_solution(6969117120376208461)
XLA Ops:
  0.6 1.4 fusion.2
  4.6 204.5 %conditional.2 = ((f32[2,2,128,4096]{3,2,1,0:T(8,128)}, f32[2,2,128,4096]{3,2,1,0:T(8,128)}, bf16[1,8,128,4096]{3,2,1,0:T(8,128)(2,1)})) conditional(s32[]{:T(128)} %bitcast.16, (s32[4,8]{1,0:T(4,128)}, s32[4]{0:T(128)}, bf16[1,192,2048]{2,1,0:T(8,128)(2,1)}, bf16[1,192,2048]{2,1,0:T(8,128)(2,1)}, bf16[1,8,128,4096]{3,2,1,0:T(8,128)(2,1)}, ...), branch_computations={%region_0.5_spmd, %region_5.6_spmd} | conditional | flops 51759808512 | bytes 295699296 | solution.py:1245
  4.8 129.0 %survivors.3 = (bf16[2,256,4096]{2,1,0:T(8,128)(2,1)}, bf16[512,4096]{1,0:T(8,128)(2,1)}, bf16[2,256,4096]{2,1,0:T(8,128)(2,1)}) custom-call(s32[4,8]{1,0:T(4,128)} %get-tuple-element.226.member_ref, s32[4]{0:T(128)} %get-tuple-element.176.flags_ref, bf16[192,2048]{1,0:T(8,128)(2,1)} %bitcast.27, bf16[192,2048]{1,0:T(8,128)(2,1)} %bitcast.29, ...), custom_call_target="tpu_custom_call" | custom-call | flops 25769803776 | bytes 33554432 | tf_op jit(solution)/shard_map/cond/branch_1_fun/survivors/pallas_call | solution.py:882
  133.8 8.5 %branch_1_fun.28 = (f32[2,2,128,4096]{3,2,1,0:T(8,128)}, f32[2,2,128,4096]{3,2,1,0:T(8,128)}, bf16[1,8,128,4096]{3,2,1,0:T(8,128)(2,1)}, bf16[128,4096]{1,0:T(8,128)(2,1)}, bf16[128,4096]{1,0:T(8,128)(2,1)}) custom-call(s32[4,8]{1,0:T(4,128)} %get-tuple-element.226.member_ref, s32[4]{0:T(128)} %get-tuple-element.176.flags_ref, s32[1]{0:T(128)} %bitcast.10.spot_ref, ...), custom_call_target="tpu_custom_call" | custom-call | flops 20971520 | bytes 20971520 | tf_op jit(solution)/shard_map/cond/branch_1_fun/pallas_call | solution.py:924
  142.3 0.6 collective-permute-start.18
  142.9 8.5 %branch_1_fun.29 = (f32[2,2,128,4096]{3,2,1,0:T(8,128)}, f32[2,2,128,4096]{3,2,1,0:T(8,128)}, bf16[1,8,128,4096]{3,2,1,0:T(8,128)(2,1)}, bf16[128,4096]{1,0:T(8,128)(2,1)}, bf16[128,4096]{1,0:T(8,128)(2,1)}) custom-call(s32[4,8]{1,0:T(4,128)} %get-tuple-element.226.member_ref, ...), custom_call_target="tpu_custom_call", output_to_operand_aliasing={{0}: (6, {}), {1}: (7, {}), {2}: (8, {})} | custom-call | flops 46137344 | bytes 46137344 | tf_op jit(solution)/shard_map/cond/branch_1_fun/pallas_call | solution.py:924
  151.4 1.4 collective-permute-start.16
  152.9 0.0 collective-permute-start.21
  152.9 0.5 collective-permute-start.20
  153.4 15.3 %collective-permute-done.18.late_ref = bf16[128,4096]{1,0:T(8,128)(2,1)} collective-permute-done((bf16[128,4096]{1,0:T(8,128)(2,1)}, bf16[128,4096]{1,0:T(8,128)(2,1)}, u32[]{:S(2)}, u32[]{:S(2)}) %collective-permute-start.18) | collective-permute-done | bytes 1048608 | tf_op jit(solution)/shard_map/cond/branch_1_fun/ppermute | solution.py:1184
  168.6 0.0 collective-permute-start.19
  168.7 20.8 %collective-permute-done.16.late_ref = bf16[128,4096]{1,0:T(8,128)(2,1)} collective-permute-done((bf16[128,4096]{1,0:T(8,128)(2,1)}, bf16[128,4096]{1,0:T(8,128)(2,1)}, u32[]{:S(2)}, u32[]{:S(2)}) %collective-permute-start.16) | collective-permute-done | bytes 1048608 | tf_op jit(solution)/shard_map/cond/branch_1_fun/ppermute | solution.py:1184
  189.4 0.0 collective-permute-start.17
  189.4 0.0 collective-permute-done.21.block_ref
  189.4 2.8 %branch_1_fun.30._ = bf16[1,8,128,4096]{3,2,1,0:T(8,128)(2,1)} custom-call(s32[4,8]{1,0:T(4,128)} %get-tuple-element.226.member_ref, s32[4]{0:T(128)} %get-tuple-element.176.flags_ref, s32[1]{0:T(128)} %bitcast.10.spot_ref, bf16[128,4096]{1,0:T(8,128)(2,1)} %collective-permute-done.21.block_ref, ...), custom_call_target="tpu_custom_call", output_to_operand_aliasing={{}: (4, {})} | custom-call | flops 9437184 | bytes 9437184 | tf_op jit(solution)/shard_map/cond/branch_1_fun/pallas_call | solution.py:924
  192.2 0.0 collective-permute-done.20.block_ref
  192.2 2.7 %branch_1_fun.31.refs_0_ = bf16[1,8,128,4096]{3,2,1,0:T(8,128)(2,1)} custom-call(s32[4,8]{1,0:T(4,128)} %get-tuple-element.226.member_ref, s32[4]{0:T(128)} %get-tuple-element.176.flags_ref, s32[1]{0:T(128)} %bitcast.10.spot_ref, bf16[128,4096]{1,0:T(8,128)(2,1)} %collective-permute-done.20.block_ref, ...), custom_call_target="tpu_custom_call", output_to_operand_aliasing={{}: (4, {})} | custom-call | flops 9437184 | bytes 9437184 | tf_op jit(solution)/shard_map/cond/branch_1_fun/pallas_call | solution.py:924
  194.9 3.5 %branch_1_fun.32.refs_0_ = bf16[1,8,128,4096]{3,2,1,0:T(8,128)(2,1)} custom-call(s32[4,8]{1,0:T(4,128)} %get-tuple-element.226.member_ref, s32[4]{0:T(128)} %get-tuple-element.176.flags_ref, s32[1]{0:T(128)} %bitcast.10.spot_ref, bf16[128,4096]{1,0:T(8,128)(2,1)} %collective-permute-done.18.late_ref, ...), custom_call_target="tpu_custom_call", output_to_operand_aliasing={{}: (6, {})} | custom-call | flops 17825792 | bytes 17825792 | tf_op jit(solution)/shard_map/cond/branch_1_fun/pallas_call | solution.py:924
  198.5 0.0 collective-permute-done.19.late_ref
  198.5 3.5 %branch_1_fun.33.refs_0_ = bf16[1,8,128,4096]{3,2,1,0:T(8,128)(2,1)} custom-call(s32[4,8]{1,0:T(4,128)} %get-tuple-element.226.member_ref, s32[4]{0:T(128)} %get-tuple-element.176.flags_ref, s32[1]{0:T(128)} %bitcast.10.spot_ref, bf16[128,4096]{1,0:T(8,128)(2,1)} %collective-permute-done.19.late_ref, ...), custom_call_target="tpu_custom_call", output_to_operand_aliasing={{}: (6, {})} | custom-call | flops 17825792 | bytes 17825792 | tf_op jit(solution)/shard_map/cond/branch_1_fun/pallas_call | solution.py:924
  202.0 3.5 %branch_1_fun.34.refs_0_ = bf16[1,8,128,4096]{3,2,1,0:T(8,128)(2,1)} custom-call(s32[4,8]{1,0:T(4,128)} %get-tuple-element.226.member_ref, s32[4]{0:T(128)} %get-tuple-element.176.flags_ref, s32[1]{0:T(128)} %bitcast.10.spot_ref, bf16[128,4096]{1,0:T(8,128)(2,1)} %collective-permute-done.16.late_ref, ...), custom_call_target="tpu_custom_call", output_to_operand_aliasing={{}: (6, {})} | custom-call | flops 17825792 | bytes 17825792 | tf_op jit(solution)/shard_map/cond/branch_1_fun/pallas_call | solution.py:924
  205.5 0.0 collective-permute-done.17.late_ref
  205.5 3.5 %branch_1_fun.35 = bf16[1,8,128,4096]{3,2,1,0:T(8,128)(2,1)} custom-call(s32[4,8]{1,0:T(4,128)} %get-tuple-element.226.member_ref, s32[4]{0:T(128)} %get-tuple-element.176.flags_ref, s32[1]{0:T(128)} %bitcast.10.spot_ref, bf16[128,4096]{1,0:T(8,128)(2,1)} %collective-permute-done.17.late_ref, ...), custom_call_target="tpu_custom_call", output_to_operand_aliasing={{}: (6, {})} | custom-call | flops 17825792 | bytes 17825792 | tf_op jit(solution)/shard_map/cond/branch_1_fun/pallas_call | solution.py:924
Async XLA Ops:
  142.3 26.3 %collective-permute-start.18 = (bf16[128,4096]{1,0:T(8,128)(2,1)}, bf16[128,4096]{1,0:T(8,128)(2,1)}, u32[]{:S(2)}, u32[]{:S(2)}) collective-permute-start(bf16[128,4096]{1,0:T(8,128)(2,1)} %get-tuple-element.194), channel_id=1, source_target_pairs={{0,16},{8,24},{16,0},{24,8},{1,17},{9,25},{17,1},{25,9},{2,18},{10... | collective-permute-start | bytes 3145736 | tf_op jit(solution)/shard_map/cond/branch_1_fun/ppermute | solution.py:1184
  151.4 38.0 %collective-permute-start.16 = (bf16[128,4096]{1,0:T(8,128)(2,1)}, bf16[128,4096]{1,0:T(8,128)(2,1)}, u32[]{:S(2)}, u32[]{:S(2)}) collective-permute-start(bf16[128,4096]{1,0:T(8,128)(2,1)} %get-tuple-element.191), channel_id=1, source_target_pairs={{0,16},{8,24},{16,0},{24,8},{1,17},{9,25},{17,1},{25,9},{2,18},{10... | collective-permute-start | bytes 3145736 | tf_op jit(solution)/shard_map/cond/branch_1_fun/ppermute | solution.py:1184
  152.9 36.6 %collective-permute-start.21 = (bf16[128,4096]{1,0:T(8,128)(2,1)}, bf16[128,4096]{1,0:T(8,128)(2,1)}, u32[]{:S(2)}, u32[]{:S(2)}) collective-permute-start(bf16[128,4096]{1,0:T(8,128)(2,1)} %get-tuple-element.196), channel_id=1, source_target_pairs={{0,8},{8,0},{16,24},{24,16},{1,9},{9,1},{17,25},{25,17},{2,10},{10... | collective-permute-start | bytes 3145736 | tf_op jit(solution)/shard_map/cond/branch_1_fun/ppermute | solution.py:1186
  152.9 39.3 %collective-permute-start.20 = (bf16[128,4096]{1,0:T(8,128)(2,1)}, bf16[128,4096]{1,0:T(8,128)(2,1)}, u32[]{:S(2)}, u32[]{:S(2)}) collective-permute-start(bf16[128,4096]{1,0:T(8,128)(2,1)} %get-tuple-element.195), channel_id=1, source_target_pairs={{0,8},{8,0},{16,24},{24,16},{1,9},{9,1},{17,25},{25,17},{2,10},{10... | collective-permute-start | bytes 3145736 | tf_op jit(solution)/shard_map/cond/branch_1_fun/ppermute | solution.py:1186
  168.6 29.8 %collective-permute-start.19 = (bf16[128,4096]{1,0:T(8,128)(2,1)}, bf16[128,4096]{1,0:T(8,128)(2,1)}, u32[]{:S(2)}, u32[]{:S(2)}) collective-permute-start(bf16[128,4096]{1,0:T(8,128)(2,1)} %collective-permute-done.18.late_ref), channel_id=1, source_target_pairs={{0,8},{8,0},{16,24},{24,16},{1,9},{9,1},{17,25},{25,17},{2,10},{10... | collective-permute-start | bytes 3145736 | tf_op jit(solution)/shard_map/cond/branch_1_fun/ppermute | solution.py:1185
  189.4 16.1 %collective-permute-start.17 = (bf16[128,4096]{1,0:T(8,128)(2,1)}, bf16[128,4096]{1,0:T(8,128)(2,1)}, u32[]{:S(2)}, u32[]{:S(2)}) collective-permute-start(bf16[128,4096]{1,0:T(8,128)(2,1)} %collective-permute-done.16.late_ref), channel_id=1, source_target_pairs={{0,8},{8,0},{16,24},{24,16},{1,9},{9,1},{17,25},{25,17},{2,10},{10... | collective-permute-start | bytes 3145736 | tf_op jit(solution)/shard_map/cond/branch_1_fun/ppermute | solution.py:1185

commit v3 on v2

--- a/solution.py
+++ b/solution.py
@@ -747,9 +747,13 @@
         share_copy(index, 1).start()
         own_copy(index).start()
 
-        @pl.when(index > 0)
+        @pl.when((index > 0) & (index % tiles != 1))
         def _():
             pick(index - 1)
+
+        @pl.when(index % tiles == 0)
+        def _():
+            pick(index)
 
         return carry
 

time: 210 us -> 210 us (level)
  no operation moved by 1% of the time
where the time goes in v3:
time: 210 us
  Pallas kernels  165 us (79%)
  waiting for transfers between devices  36.8 us (18%)
  between operations  3.21 us (2%)
  starting transfers between devices  2.54 us (1%)
    pallas_call x1, Pallas kernels, run_survivors(): pl.pallas_call(functools.partial(survivor_kernel, plan, rounds), out_shap...  129 us
    ppermute x2, waiting for transfers between devices, exchange(): sent = lax.ppermute(late_block, 'path', cross)  36.8 us
    pallas_call x8, Pallas kernels, local_call(): pl.pallas_call(body, grid_spec=pltpu.PrefetchScalarGridSpec(num_scalar_pr...  36.6 us
  transfers between devices with their start and end apart: 6, of which 2 were waited for; matrix products, arithmetic and copies ran while one was open for 0% of the time, Pallas kernels for 12%

profile of v3, /device:TPU:0, one launch (start us, length us, event | category | flops | bytes accessed | tf_op | source)
XLA Modules:
  0.0 209.6 jit_solution(1095832556257693549)
XLA Ops:
  0.6 1.4 fusion.2
  4.6 205.0 %conditional.2 = ((f32[2,2,128,4096]{3,2,1,0:T(8,128)}, f32[2,2,128,4096]{3,2,1,0:T(8,128)}, bf16[1,8,128,4096]{3,2,1,0:T(8,128)(2,1)})) conditional(s32[]{:T(128)} %bitcast.16, (s32[4,8]{1,0:T(4,128)}, s32[4]{0:T(128)}, bf16[1,192,2048]{2,1,0:T(8,128)(2,1)}, bf16[1,192,2048]{2,1,0:T(8,128)(2,1)}, bf16[1,8,128,4096]{3,2,1,0:T(8,128)(2,1)}, ...), branch_computations={%region_0.5_spmd, %region_5.6_spmd} | conditional | flops 51759808512 | bytes 295699296 | solution.py:1249
  4.8 128.7 %survivors.3 = (bf16[2,256,4096]{2,1,0:T(8,128)(2,1)}, bf16[512,4096]{1,0:T(8,128)(2,1)}, bf16[2,256,4096]{2,1,0:T(8,128)(2,1)}) custom-call(s32[4,8]{1,0:T(4,128)} %get-tuple-element.226.member_ref, s32[4]{0:T(128)} %get-tuple-element.176.flags_ref, bf16[192,2048]{1,0:T(8,128)(2,1)} %bitcast.27, bf16[192,2048]{1,0:T(8,128)(2,1)} %bitcast.29, ...), custom_call_target="tpu_custom_call" | custom-call | flops 25769803776 | bytes 33554432 | tf_op jit(solution)/shard_map/cond/branch_1_fun/survivors/pallas_call | solution.py:886
  133.6 8.5 %branch_1_fun.28 = (f32[2,2,128,4096]{3,2,1,0:T(8,128)}, f32[2,2,128,4096]{3,2,1,0:T(8,128)}, bf16[1,8,128,4096]{3,2,1,0:T(8,128)(2,1)}, bf16[128,4096]{1,0:T(8,128)(2,1)}, bf16[128,4096]{1,0:T(8,128)(2,1)}) custom-call(s32[4,8]{1,0:T(4,128)} %get-tuple-element.226.member_ref, s32[4]{0:T(128)} %get-tuple-element.176.flags_ref, s32[1]{0:T(128)} %bitcast.10.spot_ref, ...), custom_call_target="tpu_custom_call" | custom-call | flops 20971520 | bytes 20971520 | tf_op jit(solution)/shard_map/cond/branch_1_fun/pallas_call | solution.py:928
  142.1 0.5 collective-permute-start.18
  142.6 8.5 %branch_1_fun.29 = (f32[2,2,128,4096]{3,2,1,0:T(8,128)}, f32[2,2,128,4096]{3,2,1,0:T(8,128)}, bf16[1,8,128,4096]{3,2,1,0:T(8,128)(2,1)}, bf16[128,4096]{1,0:T(8,128)(2,1)}, bf16[128,4096]{1,0:T(8,128)(2,1)}) custom-call(s32[4,8]{1,0:T(4,128)} %get-tuple-element.226.member_ref, ...), custom_call_target="tpu_custom_call", output_to_operand_aliasing={{0}: (6, {}), {1}: (7, {}), {2}: (8, {})} | custom-call | flops 46137344 | bytes 46137344 | tf_op jit(solution)/shard_map/cond/branch_1_fun/pallas_call | solution.py:928
  151.1 1.5 collective-permute-start.16
  152.6 0.0 collective-permute-start.21
  152.6 0.5 collective-permute-start.20
  153.1 15.3 %collective-permute-done.18.late_ref = bf16[128,4096]{1,0:T(8,128)(2,1)} collective-permute-done((bf16[128,4096]{1,0:T(8,128)(2,1)}, bf16[128,4096]{1,0:T(8,128)(2,1)}, u32[]{:S(2)}, u32[]{:S(2)}) %collective-permute-start.18) | collective-permute-done | bytes 1048608 | tf_op jit(solution)/shard_map/cond/branch_1_fun/ppermute | solution.py:1188
  168.4 0.0 collective-permute-start.19
  168.4 21.6 %collective-permute-done.16.late_ref = bf16[128,4096]{1,0:T(8,128)(2,1)} collective-permute-done((bf16[128,4096]{1,0:T(8,128)(2,1)}, bf16[128,4096]{1,0:T(8,128)(2,1)}, u32[]{:S(2)}, u32[]{:S(2)}) %collective-permute-start.16) | collective-permute-done | bytes 1048608 | tf_op jit(solution)/shard_map/cond/branch_1_fun/ppermute | solution.py:1188
  190.0 0.0 collective-permute-start.17
  190.0 0.0 collective-permute-done.21.block_ref
  190.0 2.8 %branch_1_fun.30._ = bf16[1,8,128,4096]{3,2,1,0:T(8,128)(2,1)} custom-call(s32[4,8]{1,0:T(4,128)} %get-tuple-element.226.member_ref, s32[4]{0:T(128)} %get-tuple-element.176.flags_ref, s32[1]{0:T(128)} %bitcast.10.spot_ref, bf16[128,4096]{1,0:T(8,128)(2,1)} %collective-permute-done.21.block_ref, ...), custom_call_target="tpu_custom_call", output_to_operand_aliasing={{}: (4, {})} | custom-call | flops 9437184 | bytes 9437184 | tf_op jit(solution)/shard_map/cond/branch_1_fun/pallas_call | solution.py:928
  192.7 0.0 collective-permute-done.20.block_ref
  192.7 2.7 %branch_1_fun.31.refs_0_ = bf16[1,8,128,4096]{3,2,1,0:T(8,128)(2,1)} custom-call(s32[4,8]{1,0:T(4,128)} %get-tuple-element.226.member_ref, s32[4]{0:T(128)} %get-tuple-element.176.flags_ref, s32[1]{0:T(128)} %bitcast.10.spot_ref, bf16[128,4096]{1,0:T(8,128)(2,1)} %collective-permute-done.20.block_ref, ...), custom_call_target="tpu_custom_call", output_to_operand_aliasing={{}: (4, {})} | custom-call | flops 9437184 | bytes 9437184 | tf_op jit(solution)/shard_map/cond/branch_1_fun/pallas_call | solution.py:928
  195.5 3.5 %branch_1_fun.32.refs_0_ = bf16[1,8,128,4096]{3,2,1,0:T(8,128)(2,1)} custom-call(s32[4,8]{1,0:T(4,128)} %get-tuple-element.226.member_ref, s32[4]{0:T(128)} %get-tuple-element.176.flags_ref, s32[1]{0:T(128)} %bitcast.10.spot_ref, bf16[128,4096]{1,0:T(8,128)(2,1)} %collective-permute-done.18.late_ref, ...), custom_call_target="tpu_custom_call", output_to_operand_aliasing={{}: (6, {})} | custom-call | flops 17825792 | bytes 17825792 | tf_op jit(solution)/shard_map/cond/branch_1_fun/pallas_call | solution.py:928
  199.0 0.0 collective-permute-done.19.late_ref
  199.0 3.5 %branch_1_fun.33.refs_0_ = bf16[1,8,128,4096]{3,2,1,0:T(8,128)(2,1)} custom-call(s32[4,8]{1,0:T(4,128)} %get-tuple-element.226.member_ref, s32[4]{0:T(128)} %get-tuple-element.176.flags_ref, s32[1]{0:T(128)} %bitcast.10.spot_ref, bf16[128,4096]{1,0:T(8,128)(2,1)} %collective-permute-done.19.late_ref, ...), custom_call_target="tpu_custom_call", output_to_operand_aliasing={{}: (6, {})} | custom-call | flops 17825792 | bytes 17825792 | tf_op jit(solution)/shard_map/cond/branch_1_fun/pallas_call | solution.py:928
  202.5 3.5 %branch_1_fun.34.refs_0_ = bf16[1,8,128,4096]{3,2,1,0:T(8,128)(2,1)} custom-call(s32[4,8]{1,0:T(4,128)} %get-tuple-element.226.member_ref, s32[4]{0:T(128)} %get-tuple-element.176.flags_ref, s32[1]{0:T(128)} %bitcast.10.spot_ref, bf16[128,4096]{1,0:T(8,128)(2,1)} %collective-permute-done.16.late_ref, ...), custom_call_target="tpu_custom_call", output_to_operand_aliasing={{}: (6, {})} | custom-call | flops 17825792 | bytes 17825792 | tf_op jit(solution)/shard_map/cond/branch_1_fun/pallas_call | solution.py:928
  206.1 0.0 collective-permute-done.17.late_ref
  206.1 3.5 %branch_1_fun.35 = bf16[1,8,128,4096]{3,2,1,0:T(8,128)(2,1)} custom-call(s32[4,8]{1,0:T(4,128)} %get-tuple-element.226.member_ref, s32[4]{0:T(128)} %get-tuple-element.176.flags_ref, s32[1]{0:T(128)} %bitcast.10.spot_ref, bf16[128,4096]{1,0:T(8,128)(2,1)} %collective-permute-done.17.late_ref, ...), custom_call_target="tpu_custom_call", output_to_operand_aliasing={{}: (6, {})} | custom-call | flops 17825792 | bytes 17825792 | tf_op jit(solution)/shard_map/cond/branch_1_fun/pallas_call | solution.py:928
Async XLA Ops:
  142.1 26.3 %collective-permute-start.18 = (bf16[128,4096]{1,0:T(8,128)(2,1)}, bf16[128,4096]{1,0:T(8,128)(2,1)}, u32[]{:S(2)}, u32[]{:S(2)}) collective-permute-start(bf16[128,4096]{1,0:T(8,128)(2,1)} %get-tuple-element.194), channel_id=1, source_target_pairs={{0,16},{8,24},{16,0},{24,8},{1,17},{9,25},{17,1},{25,9},{2,18},{10... | collective-permute-start | bytes 3145736 | tf_op jit(solution)/shard_map/cond/branch_1_fun/ppermute | solution.py:1188
  151.1 38.9 %collective-permute-start.16 = (bf16[128,4096]{1,0:T(8,128)(2,1)}, bf16[128,4096]{1,0:T(8,128)(2,1)}, u32[]{:S(2)}, u32[]{:S(2)}) collective-permute-start(bf16[128,4096]{1,0:T(8,128)(2,1)} %get-tuple-element.191), channel_id=1, source_target_pairs={{0,16},{8,24},{16,0},{24,8},{1,17},{9,25},{17,1},{25,9},{2,18},{10... | collective-permute-start | bytes 3145736 | tf_op jit(solution)/shard_map/cond/branch_1_fun/ppermute | solution.py:1188
  152.6 37.4 %collective-permute-start.21 = (bf16[128,4096]{1,0:T(8,128)(2,1)}, bf16[128,4096]{1,0:T(8,128)(2,1)}, u32[]{:S(2)}, u32[]{:S(2)}) collective-permute-start(bf16[128,4096]{1,0:T(8,128)(2,1)} %get-tuple-element.196), channel_id=1, source_target_pairs={{0,8},{8,0},{16,24},{24,16},{1,9},{9,1},{17,25},{25,17},{2,10},{10... | collective-permute-start | bytes 3145736 | tf_op jit(solution)/shard_map/cond/branch_1_fun/ppermute | solution.py:1190
  152.6 40.1 %collective-permute-start.20 = (bf16[128,4096]{1,0:T(8,128)(2,1)}, bf16[128,4096]{1,0:T(8,128)(2,1)}, u32[]{:S(2)}, u32[]{:S(2)}) collective-permute-start(bf16[128,4096]{1,0:T(8,128)(2,1)} %get-tuple-element.195), channel_id=1, source_target_pairs={{0,8},{8,0},{16,24},{24,16},{1,9},{9,1},{17,25},{25,17},{2,10},{10... | collective-permute-start | bytes 3145736 | tf_op jit(solution)/shard_map/cond/branch_1_fun/ppermute | solution.py:1190
  168.4 30.6 %collective-permute-start.19 = (bf16[128,4096]{1,0:T(8,128)(2,1)}, bf16[128,4096]{1,0:T(8,128)(2,1)}, u32[]{:S(2)}, u32[]{:S(2)}) collective-permute-start(bf16[128,4096]{1,0:T(8,128)(2,1)} %collective-permute-done.18.late_ref), channel_id=1, source_target_pairs={{0,8},{8,0},{16,24},{24,16},{1,9},{9,1},{17,25},{25,17},{2,10},{10... | collective-permute-start | bytes 3145736 | tf_op jit(solution)/shard_map/cond/branch_1_fun/ppermute | solution.py:1189
  190.0 16.1 %collective-permute-start.17 = (bf16[128,4096]{1,0:T(8,128)(2,1)}, bf16[128,4096]{1,0:T(8,128)(2,1)}, u32[]{:S(2)}, u32[]{:S(2)}) collective-permute-start(bf16[128,4096]{1,0:T(8,128)(2,1)} %collective-permute-done.16.late_ref), channel_id=1, source_target_pairs={{0,8},{8,0},{16,24},{24,16},{1,9},{9,1},{17,25},{25,17},{2,10},{10... | collective-permute-start | bytes 3145736 | tf_op jit(solution)/shard_map/cond/branch_1_fun/ppermute | solution.py:1189
